TPU v7x, 256 devices: a whole 4x4x8 slice. The times are simulated.
256 devices in a mesh: ty: 8 (over z_lo, core), tx: 32 (over x, y, z_hi).
Axes of the slice: x: 4, y: 4, z: 8 (z_hi: 2, z_lo: 4; z = z_hi * 4 + z_lo), core: 2. Of those that a mesh axis runs over, the one named last changes fastest.
Arguments:
- movie: bfloat16 [256, 1024, 128], P('ty', 'tx'), may hold values from 0 to 2
- footprints: bfloat16 [8, 32, 32, 1024], P('ty', 'tx'), may hold values from 0.049804688 to 1
- centres: int32 [8, 32, 32, 2], P('ty', 'tx'), may hold values from 0 to 31
- traces: bfloat16 [8, 32, 32, 128], P('ty', 'tx'), may hold values from 0 to 1
- counts: int32 [8, 32], P('ty', 'tx'), may hold values from 8 to 32
- order: int32 [8, 32, 32], P('ty', 'tx'), may hold values from 0 to 31, each once within a row
Outputs:
- new_traces: float32 [8, 32, 32, 128], P('ty', 'tx')
Inputs may be any that keep to these rules, and one draw needn't show every extreme that they name: Slots 0 to counts - 1 of a tile hold neurons; the footprints, centres and traces of the other slots are not used. order[a, b] holds each of 0 to 31 once. `centres`: A centre lies inside its owner tile.
All inputs are finite; a program needn't handle non-finite values.
Results may differ from a plain program's by a relative error of at most 0.0003.
Values may be sent and summed in bfloat16 or wider, within the bound.
A program may use at most 64 MiB of HBM per device.

v0:
```python
import jax
import jax.numpy as jnp
from jax import lax
from jax.sharding import PartitionSpec as P

BLOCKS = 4
PATCH = 32


precise = lax.Precision.HIGHEST


def extended(x, sides, width):
    for axis, dim in sides:
        devices, length = (lax.axis_size(axis), x.shape[dim])
        up = [(i, (i + 1) % devices) for i in range(devices - 1)]
        down = [(j, i) for i, j in up]
        last = lax.slice_in_dim(x, length - width, length, axis=dim)
        first = lax.slice_in_dim(x, 0, width, axis=dim)
        before = lax.ppermute(last, axis, up)
        after = lax.ppermute(first, axis, down)
        x = jnp.concatenate([before, x, after], axis=dim)
    return x


def placement(anchors, extent, length):
    across = jnp.arange(extent, dtype=jnp.int32)[None, :, None]
    inside = jnp.arange(length, dtype=jnp.int32)[None, None, :]
    return (across == anchors[:, None, None] + inside).astype(jnp.bfloat16)


def paint(patches, top_rows, left_cols, canvas_rows, canvas_cols):
    rows_hot = placement(top_rows, canvas_rows, PATCH)
    cols_hot = placement(left_cols, canvas_cols, PATCH)
    spread = jnp.einsum(
        "kyi,kij->kyj", rows_hot, patches, preferred_element_type=jnp.float32
    ).astype(jnp.bfloat16)
    canvas = jnp.einsum(
        "kyj,kxj->kyx", spread, cols_hot, preferred_element_type=jnp.float32
    ).astype(jnp.bfloat16)
    return canvas.reshape(patches.shape[0], canvas_rows * canvas_cols)


def body(movie, footprints, centres, traces, counts, order):
    tile_side = movie.shape[0]
    frame_count = movie.shape[2]
    slot_count = footprints.shape[2]
    half_patch = PATCH // 2
    block_rows = slot_count // BLOCKS
    ordering = order[0, 0]
    alive_mask = ordering < counts[0, 0]
    selector = ordering[:, None] == jnp.arange(slot_count, dtype=jnp.int32)[None, :]
    chooser = (selector & alive_mask[:, None]).astype(jnp.bfloat16)
    own_flat = jnp.dot(chooser, footprints[0, 0], preferred_element_type=jnp.float32).astype(
        jnp.bfloat16
    )
    first_traces = jnp.dot(chooser, traces[0, 0], preferred_element_type=jnp.float32).astype(
        jnp.bfloat16
    )
    picker = selector.astype(jnp.int32)
    own_pos = jnp.sum(picker[:, :, None] * centres[0, 0][None, :, :], axis=1)
    near_flat, near_pos, near_traces = (
        extended(own_flat[None, None], (("ty", 0), ("tx", 1)), 1),
        extended(own_pos.astype(jnp.bfloat16)[None, None], (("ty", 0), ("tx", 1)), 1),
        extended(first_traces[None, None], (("ty", 0), ("tx", 1)), 1),
    )
    offsets = (jnp.arange(3, dtype=jnp.int32) - 1) * tile_side
    near_rows = (near_pos[..., 0].astype(jnp.int32) + offsets[:, None, None]).reshape(
        9 * slot_count
    )
    near_cols = (near_pos[..., 1].astype(jnp.int32) + offsets[None, :, None]).reshape(
        9 * slot_count
    )
    own_rows = own_pos[:, 0]
    own_cols = own_pos[:, 1]
    own_patch = own_flat.reshape(slot_count, PATCH, PATCH)
    near_patch = near_flat.reshape(9 * slot_count, PATCH, PATCH)
    canvas_side = tile_side + 2 * half_patch
    own_canvas = paint(own_patch, own_rows, own_cols, canvas_side, canvas_side)
    near_canvas = paint(near_patch, near_rows, near_cols, canvas_side, canvas_side)
    margins = lax.dot_general(
        own_canvas, near_canvas, (((1,), (1,)), ((), ())), preferred_element_type=jnp.float32
    )
    by_source = margins.reshape(slot_count, 9, slot_count)
    padded_movie = extended(movie, (("ty", 0), ("tx", 1)), half_patch)
    drive_term = jnp.dot(
        own_canvas,
        padded_movie.reshape(canvas_side * canvas_side, frame_count),
        preferred_element_type=jnp.float32,
    )
    current = first_traces.astype(jnp.float32)
    coupling = jnp.dot(
        margins,
        near_traces.reshape(9 * slot_count, frame_count).astype(jnp.float32),
        precision=precise,
        preferred_element_type=jnp.float32,
    )
    diagonal = jnp.diagonal(by_source[:, 4])
    denominator = jnp.where(alive_mask, diagonal, 1.0)
    for block_index in range(BLOCKS):
        lower = block_index * block_rows
        upper = lower + block_rows
        previous = current[lower:upper]
        renewed = jnp.maximum(
            previous
            + (drive_term[lower:upper] - coupling[lower:upper]) / denominator[lower:upper, None],
            0.0,
        )
        renewed = jnp.where(alive_mask[lower:upper, None], renewed, 0.0)
        current = current.at[lower:upper].set(renewed)
        if block_index + 1 < BLOCKS:
            change = extended((renewed - previous)[None, None], (("ty", 0), ("tx", 1)), 1)
            columns = by_source[:, :, lower:upper].reshape(slot_count, 9 * block_rows)
            coupling = coupling + jnp.dot(
                columns,
                change.reshape(9 * block_rows, frame_count),
                precision=precise,
                preferred_element_type=jnp.float32,
            )
    result = lax.dot_general(
        selector.astype(jnp.float32),
        current,
        (((0,), (0,)), ((), ())),
        precision=precise,
        preferred_element_type=jnp.float32,
    )
    return result[None, None]


def solution(mesh):
    in_specs = (
        P("ty", "tx", None),
        P("ty", "tx", None, None),
        P("ty", "tx", None, None),
        P("ty", "tx", None, None),
        P("ty", "tx"),
        P("ty", "tx", None),
    )
    out_specs = P("ty", "tx", None, None)
    return jax.shard_map(body, mesh=mesh, in_specs=in_specs, out_specs=out_specs, check_vma=False)
```

profile of v0, /device:TPU:7, one launch (start us, length us, event | category | flops | bytes accessed | tf_op | source)
XLA Modules:
  0.0 184.6 jit_solution(1787720312205405255)
XLA Ops:
  0.7 0.7 broadcast_compare_fusion
  1.4 0.9 convolution_convert_fusion.2
  2.2 4.1 %collective-permute-start.8 = (bf16[1,1,32,1024]{3,2,1,0:T(8,128)(2,1)S(1)}, bf16[1,1,32,1024]{3,2,1,0:T(8,128)(2,1)S(1)}, u32[]{:S(2)}, u32[]{:S(2)}) collective-permute-start(bf16[1,1,32,1024]{3,2,1,0:T(8,128)(2,1)S(1)} %bitcast.65), channel_id=1, source_target_pairs={{0,32},{32,64},{64,96},{96,128},{128,160},{160,192},{192,224},{1,3... | collective-permute-start | bytes 196616 | tf_op jit(solution)/shard_map/ppermute | solution.py:20
  6.3 1.9 %collective-permute-start.9 = (bf16[1,1,32,1024]{3,2,1,0:T(8,128)(2,1)S(1)}, bf16[1,1,32,1024]{3,2,1,0:T(8,128)(2,1)S(1)}, u32[]{:S(2)}, u32[]{:S(2)}) collective-permute-start(bf16[1,1,32,1024]{3,2,1,0:T(8,128)(2,1)S(1)} %bitcast.66), channel_id=1, source_target_pairs={{32,0},{64,32},{96,64},{128,96},{160,128},{192,160},{224,192},{33,... | collective-permute-start | bytes 196616 | tf_op jit(solution)/shard_map/ppermute | solution.py:21
  8.3 0.7 fusion.23
  9.0 0.8 multiply_reduce_fusion
  9.8 3.6 %collective-permute-start.4 = (bf16[1,1,32,2]{2,3,1,0:T(2,128)(2,1)S(1)}, bf16[1,1,32,2]{2,3,1,0:T(2,128)(2,1)S(1)}, u32[]{:S(2)}, u32[]{:S(2)}) collective-permute-start(bf16[1,1,32,2]{2,3,1,0:T(2,128)(2,1)S(1)} %convert_bitcast_fusion), channel_id=1, source_target_pairs={{0,32},{32,64},{64,96},{96,128},{128,160},{160,192},{192,224},{1,3... | collective-permute-start | bytes 392 | tf_op jit(solution)/shard_map/ppermute | solution.py:20
  13.4 1.9 %collective-permute-start.5 = (bf16[1,1,32,2]{2,3,1,0:T(2,128)(2,1)S(1)}, bf16[1,1,32,2]{2,3,1,0:T(2,128)(2,1)S(1)}, u32[]{:S(2)}, u32[]{:S(2)}) collective-permute-start(bf16[1,1,32,2]{2,3,1,0:T(2,128)(2,1)S(1)} %convert_bitcast_fusion), channel_id=1, source_target_pairs={{32,0},{64,32},{96,64},{128,96},{160,128},{192,160},{224,192},{33,... | collective-permute-start | bytes 392 | tf_op jit(solution)/shard_map/ppermute | solution.py:21
  15.4 1.5 fusion.61
  16.9 3.6 %collective-permute-start.12 = (bf16[1,1,32,128]{3,2,1,0:T(8,128)(2,1)S(1)}, bf16[1,1,32,128]{3,2,1,0:T(8,128)(2,1)S(1)}, u32[]{:S(2)}, u32[]{:S(2)}) collective-permute-start(bf16[1,1,32,128]{3,2,1,0:T(8,128)(2,1)S(1)} %bitcast.77), channel_id=1, source_target_pairs={{0,32},{32,64},{64,96},{96,128},{128,160},{160,192},{192,224},{1,3... | collective-permute-start | bytes 24584 | tf_op jit(solution)/shard_map/ppermute | solution.py:20
  20.5 0.2 reshape.303
  20.7 0.5 fusion.59
  21.2 1.0 fusion.58
  22.3 1.8 convolution_convert_fusion
  24.1 7.9 %collective-permute-start.6 = (bf16[3,1,32,2]{2,3,1,0:T(2,128)(2,1)S(1)}, bf16[3,1,32,2]{2,3,1,0:T(2,128)(2,1)S(1)}, u32[]{:S(2)}, u32[]{:S(2)}) collective-permute-start(bf16[3,1,32,2]{2,3,1,0:T(2,128)(2,1)S(1)} %pad_maximum_fusion.11), channel_id=1, source_target_pairs={{0,1},{1,2},{2,3},{3,4},{4,5},{5,6},{6,7},{7,8},{8,9},{9,10},{10,1... | collective-permute-start | bytes 1160 | tf_op jit(solution)/shard_map/ppermute | solution.py:20
  32.1 4.6 %collective-permute-start.7 = (bf16[3,1,32,2]{2,3,1,0:T(2,128)(2,1)S(1)}, bf16[3,1,32,2]{2,3,1,0:T(2,128)(2,1)S(1)}, u32[]{:S(2)}, u32[]{:S(2)}) collective-permute-start(bf16[3,1,32,2]{2,3,1,0:T(2,128)(2,1)S(1)} %pad_maximum_fusion.11), channel_id=1, source_target_pairs={{1,0},{2,1},{3,2},{4,3},{5,4},{6,5},{7,6},{8,7},{9,8},{10,9},{11,1... | collective-permute-start | bytes 1160 | tf_op jit(solution)/shard_map/ppermute | solution.py:21
  36.8 0.1 add.155
  36.9 0.1 add.161
  37.0 1.9 %collective-permute-start.13 = (bf16[1,1,32,128]{3,2,1,0:T(8,128)(2,1)S(1)}, bf16[1,1,32,128]{3,2,1,0:T(8,128)(2,1)S(1)}, u32[]{:S(2)}, u32[]{:S(2)}) collective-permute-start(bf16[1,1,32,128]{3,2,1,0:T(8,128)(2,1)S(1)} %bitcast.78), channel_id=1, source_target_pairs={{32,0},{64,32},{96,64},{128,96},{160,128},{192,160},{224,192},{33,... | collective-permute-start | bytes 24584 | tf_op jit(solution)/shard_map/ppermute | solution.py:21
  39.0 1.3 collective-permute-done.7
  40.3 3.3 %collective-permute-start = (bf16[16,32,128]{2,1,0:T(8,128)(2,1)S(1)}, bf16[16,32,128]{2,1,0:T(8,128)(2,1)S(1)}, u32[]{:S(2)}, u32[]{:S(2)}) collective-permute-start(bf16[16,32,128]{2,1,0:T(8,128)(2,1)S(1)} %get-tuple-element.64), channel_id=1, source_target_pairs={{0,32},{32,64},{64,96},{96,128},{128,160},{160,192},{192,224},{1,3... | collective-permute-start | bytes 393224 | tf_op jit(solution)/shard_map/ppermute | solution.py:20
  43.8 0.4 iota_compare_fusion.2
  44.2 0.1 reshape.314
  44.3 3.5 %collective-permute-start.14 = (bf16[3,1,32,128]{3,2,1,0:T(8,128)(2,1)S(1)}, bf16[3,1,32,128]{3,2,1,0:T(8,128)(2,1)S(1)}, u32[]{:S(2)}, u32[]{:S(2)}) collective-permute-start(bf16[3,1,32,128]{3,2,1,0:T(8,128)(2,1)S(1)} %pad_maximum_fusion.6), channel_id=1, source_target_pairs={{0,1},{1,2},{2,3},{3,4},{4,5},{5,6},{6,7},{7,8},{8,9},{9,10},{10,1... | collective-permute-start | bytes 73736 | tf_op jit(solution)/shard_map/ppermute | solution.py:20
  47.9 8.7 %collective-permute-start.15 = (bf16[3,1,32,128]{3,2,1,0:T(8,128)(2,1)S(1)}, bf16[3,1,32,128]{3,2,1,0:T(8,128)(2,1)S(1)}, u32[]{:S(2)}, u32[]{:S(2)}) collective-permute-start(bf16[3,1,32,128]{3,2,1,0:T(8,128)(2,1)S(1)} %pad_maximum_fusion.6), channel_id=1, source_target_pairs={{1,0},{2,1},{3,2},{4,3},{5,4},{6,5},{7,6},{8,7},{9,8},{10,9},{11,1... | collective-permute-start | bytes 73736 | tf_op jit(solution)/shard_map/ppermute | solution.py:21
  56.5 0.8 iota_add_fusion
  57.3 6.4 %copy.17 = pred[288,64,32]{1,2,0:T(32,128)(4,1)} copy(pred[288,64,32]{0,2,1:T(32,128)(4,1)S(1)} %iota_compare_fusion.2) | data formatting | bytes 1179648 | tf_op jit(solution)/shard_map/eq | solution.py:29
  63.7 1.9 %collective-permute-start.1 = (bf16[16,32,128]{2,1,0:T(8,128)(2,1)S(1)}, bf16[16,32,128]{2,1,0:T(8,128)(2,1)S(1)}, u32[]{:S(2)}, u32[]{:S(2)}) collective-permute-start(bf16[16,32,128]{2,1,0:T(8,128)(2,1)S(1)} %get-tuple-element.63), channel_id=1, source_target_pairs={{32,0},{64,32},{96,64},{128,96},{160,128},{192,160},{224,192},{33,... | collective-permute-start | bytes 393224 | tf_op jit(solution)/shard_map/ppermute | solution.py:21
  65.7 0.6 pad_maximum_fusion.2
  66.4 1.9 %collective-permute-start.10 = (bf16[3,1,32,1024]{3,2,1,0:T(8,128)(2,1)S(1)}, bf16[3,1,32,1024]{3,2,1,0:T(8,128)(2,1)S(1)}, u32[]{:S(2)}, u32[]{:S(2)}) collective-permute-start(bf16[3,1,32,1024]{3,2,1,0:T(8,128)(2,1)S(1)} %pad_maximum_fusion.1), channel_id=1, source_target_pairs={{0,1},{1,2},{2,3},{3,4},{4,5},{5,6},{6,7},{7,8},{8,9},{9,10},{10,1... | collective-permute-start | bytes 589832 | tf_op jit(solution)/shard_map/ppermute | solution.py:20
  68.3 10.3 %collective-permute-start.11 = (bf16[3,1,32,1024]{3,2,1,0:T(8,128)(2,1)S(1)}, bf16[3,1,32,1024]{3,2,1,0:T(8,128)(2,1)S(1)}, u32[]{:S(2)}, u32[]{:S(2)}) collective-permute-start(bf16[3,1,32,1024]{3,2,1,0:T(8,128)(2,1)S(1)} %pad_maximum_fusion.1), channel_id=1, source_target_pairs={{1,0},{2,1},{3,2},{4,3},{5,4},{6,5},{7,6},{8,7},{9,8},{10,9},{11,1... | collective-permute-start | bytes 589832 | tf_op jit(solution)/shard_map/ppermute | solution.py:21
  78.7 0.8 fusion.57
  79.5 1.9 %collective-permute-start.2 = (bf16[64,16,128]{2,1,0:T(8,128)(2,1)}, bf16[64,16,128]{2,1,0:T(8,128)(2,1)}, u32[]{:S(2)}, u32[]{:S(2)}) collective-permute-start(bf16[64,16,128]{2,1,0:T(8,128)(2,1)} %get-tuple-element.61), channel_id=1, source_target_pairs={{0,1},{1,2},{2,3},{3,4},{4,5},{5,6},{6,7},{7,8},{8,9},{9,10},{10,1... | collective-permute-start | bytes 786440 | tf_op jit(solution)/shard_map/ppermute | solution.py:20
  81.4 10.5 %collective-permute-start.3 = (bf16[64,16,128]{2,1,0:T(8,128)(2,1)}, bf16[64,16,128]{2,1,0:T(8,128)(2,1)}, u32[]{:S(2)}, u32[]{:S(2)}) collective-permute-start(bf16[64,16,128]{2,1,0:T(8,128)(2,1)} %get-tuple-element.62), channel_id=1, source_target_pairs={{1,0},{2,1},{3,2},{4,3},{5,4},{6,5},{7,6},{8,7},{9,8},{10,9},{11,1... | collective-permute-start | bytes 786440 | tf_op jit(solution)/shard_map/ppermute | solution.py:21
  92.0 1.8 reshape.304
  93.8 6.5 %fusion.3 = bf16[288,64,64]{2,1,0:T(8,128)(2,1)} fusion(s32[288,32]{1,0:T(8,128)} %iota_add_fusion, pred[288,64,32]{1,2,0:T(32,128)(4,1)} %copy.17, bf16[288,32,32]{2,1,0:T(8,128)(2,1)S(1)} %reshape.304), kind=kOutput, calls=%fused_computation.6 | convolution fusion | flops 115605504 | bytes 3575808 | tf_op jit(solution)/shard_map/kyj,kxj->kyx/dot_general | solution.py:38
  100.4 5.2 %fusion.8 = f32[32,288]{1,0:T(8,128)S(1)} fusion(bf16[288,64,64]{2,1,0:T(8,128)(2,1)} %fusion.3, bf16[32,64,64]{2,1,0:T(8,128)(2,1)S(1)} %copy-done.6), kind=kOutput, calls=%fused_computation.13 | convolution fusion | flops 75497472 | bytes 2658304 | tf_op jit(solution)/shard_map/dot_general | solution.py:81
  105.6 0.1 copy.21
  105.8 0.7 gather_fusion
  106.6 0.2 fusion.62
  106.8 5.9 %collective-permute-done.3 = bf16[64,16,128]{2,1,0:T(8,128)(2,1)} collective-permute-done((bf16[64,16,128]{2,1,0:T(8,128)(2,1)}, bf16[64,16,128]{2,1,0:T(8,128)(2,1)}, u32[]{:S(2)}, u32[]{:S(2)}) %collective-permute-start.3) | collective-permute-done | bytes 262176 | tf_op jit(solution)/shard_map/ppermute | solution.py:21
  112.7 1.8 convolution_bitcast_fusion
  114.6 3.4 %collective-permute-start.16 = (f32[1,1,8,128]{3,2,1,0:T(8,128)S(1)}, f32[1,1,8,128]{3,2,1,0:T(8,128)S(1)}, u32[]{:S(2)}, u32[]{:S(2)}) collective-permute-start(f32[1,1,8,128]{3,2,1,0:T(8,128)S(1)} %get-tuple-element.59), channel_id=1, source_target_pairs={{0,32},{32,64},{64,96},{96,128},{128,160},{160,192},{192,224},{1,3... | collective-permute-start | bytes 12296 | tf_op jit(solution)/shard_map/ppermute | solution.py:20
  118.0 1.9 %collective-permute-start.17 = (f32[1,1,8,128]{3,2,1,0:T(8,128)S(1)}, f32[1,1,8,128]{3,2,1,0:T(8,128)S(1)}, u32[]{:S(2)}, u32[]{:S(2)}) collective-permute-start(f32[1,1,8,128]{3,2,1,0:T(8,128)S(1)} %get-tuple-element.59), channel_id=1, source_target_pairs={{32,0},{64,32},{96,64},{128,96},{160,128},{192,160},{224,192},{33,... | collective-permute-start | bytes 12296 | tf_op jit(solution)/shard_map/ppermute | solution.py:21
  119.9 3.0 %collective-permute-done.17 = f32[1,1,8,128]{3,2,1,0:T(8,128)S(1)} collective-permute-done((f32[1,1,8,128]{3,2,1,0:T(8,128)S(1)}, f32[1,1,8,128]{3,2,1,0:T(8,128)S(1)}, u32[]{:S(2)}, u32[]{:S(2)}) %collective-permute-start.17) | collective-permute-done | bytes 4128 | tf_op jit(solution)/shard_map/ppermute | solution.py:21
  122.9 4.0 %collective-permute-start.18 = (f32[3,1,8,128]{3,2,1,0:T(8,128)S(1)}, f32[3,1,8,128]{3,2,1,0:T(8,128)S(1)}, u32[]{:S(2)}, u32[]{:S(2)}) collective-permute-start(f32[3,1,8,128]{3,2,1,0:T(8,128)S(1)} %pad_maximum_fusion.7), channel_id=1, source_target_pairs={{0,1},{1,2},{2,3},{3,4},{4,5},{5,6},{6,7},{7,8},{8,9},{9,10},{10,1... | collective-permute-start | bytes 36872 | tf_op jit(solution)/shard_map/ppermute | solution.py:20
  127.0 8.1 %collective-permute-start.19 = (f32[3,1,8,128]{3,2,1,0:T(8,128)S(1)}, f32[3,1,8,128]{3,2,1,0:T(8,128)S(1)}, u32[]{:S(2)}, u32[]{:S(2)}) collective-permute-start(f32[3,1,8,128]{3,2,1,0:T(8,128)S(1)} %pad_maximum_fusion.7), channel_id=1, source_target_pairs={{1,0},{2,1},{3,2},{4,3},{5,4},{6,5},{7,6},{8,7},{9,8},{10,9},{11,1... | collective-permute-start | bytes 36872 | tf_op jit(solution)/shard_map/ppermute | solution.py:21
  135.2 1.5 collective-permute-done.19
  136.7 0.2 convolution_add_fusion.1
  137.0 3.1 %collective-permute-start.20 = (f32[1,1,8,128]{3,2,1,0:T(8,128)S(1)}, f32[1,1,8,128]{3,2,1,0:T(8,128)S(1)}, u32[]{:S(2)}, u32[]{:S(2)}) collective-permute-start(f32[1,1,8,128]{3,2,1,0:T(8,128)S(1)} %get-tuple-element.57), channel_id=1, source_target_pairs={{0,32},{32,64},{64,96},{96,128},{128,160},{160,192},{192,224},{1,3... | collective-permute-start | bytes 12296 | tf_op jit(solution)/shard_map/ppermute | solution.py:20
  140.1 1.9 %collective-permute-start.21 = (f32[1,1,8,128]{3,2,1,0:T(8,128)S(1)}, f32[1,1,8,128]{3,2,1,0:T(8,128)S(1)}, u32[]{:S(2)}, u32[]{:S(2)}) collective-permute-start(f32[1,1,8,128]{3,2,1,0:T(8,128)S(1)} %get-tuple-element.57), channel_id=1, source_target_pairs={{32,0},{64,32},{96,64},{128,96},{160,128},{192,160},{224,192},{33,... | collective-permute-start | bytes 12296 | tf_op jit(solution)/shard_map/ppermute | solution.py:21
  142.0 3.0 %collective-permute-done.21 = f32[1,1,8,128]{3,2,1,0:T(8,128)S(1)} collective-permute-done((f32[1,1,8,128]{3,2,1,0:T(8,128)S(1)}, f32[1,1,8,128]{3,2,1,0:T(8,128)S(1)}, u32[]{:S(2)}, u32[]{:S(2)}) %collective-permute-start.21) | collective-permute-done | bytes 4128 | tf_op jit(solution)/shard_map/ppermute | solution.py:21
  145.0 8.4 %collective-permute-start.22 = (f32[3,1,8,128]{3,2,1,0:T(8,128)S(1)}, f32[3,1,8,128]{3,2,1,0:T(8,128)S(1)}, u32[]{:S(2)}, u32[]{:S(2)}) collective-permute-start(f32[3,1,8,128]{3,2,1,0:T(8,128)S(1)} %pad_maximum_fusion.8), channel_id=1, source_target_pairs={{0,1},{1,2},{2,3},{3,4},{4,5},{5,6},{6,7},{7,8},{8,9},{9,10},{10,1... | collective-permute-start | bytes 36872 | tf_op jit(solution)/shard_map/ppermute | solution.py:20
  153.5 3.8 %collective-permute-start.23 = (f32[3,1,8,128]{3,2,1,0:T(8,128)S(1)}, f32[3,1,8,128]{3,2,1,0:T(8,128)S(1)}, u32[]{:S(2)}, u32[]{:S(2)}) collective-permute-start(f32[3,1,8,128]{3,2,1,0:T(8,128)S(1)} %pad_maximum_fusion.8), channel_id=1, source_target_pairs={{1,0},{2,1},{3,2},{4,3},{5,4},{6,5},{7,6},{8,7},{9,8},{10,9},{11,1... | collective-permute-start | bytes 36872 | tf_op jit(solution)/shard_map/ppermute | solution.py:21
  157.2 4.6 %collective-permute-done.23 = f32[3,1,8,128]{3,2,1,0:T(8,128)S(1)} collective-permute-done((f32[3,1,8,128]{3,2,1,0:T(8,128)S(1)}, f32[3,1,8,128]{3,2,1,0:T(8,128)S(1)}, u32[]{:S(2)}, u32[]{:S(2)}) %collective-permute-start.23) | collective-permute-done | bytes 12320 | tf_op jit(solution)/shard_map/ppermute | solution.py:21
  161.8 0.2 convolution_add_fusion
  162.1 3.4 %collective-permute-start.24 = (f32[1,1,8,128]{3,2,1,0:T(8,128)S(1)}, f32[1,1,8,128]{3,2,1,0:T(8,128)S(1)}, u32[]{:S(2)}, u32[]{:S(2)}) collective-permute-start(f32[1,1,8,128]{3,2,1,0:T(8,128)S(1)} %get-tuple-element.55), channel_id=1, source_target_pairs={{0,32},{32,64},{64,96},{96,128},{128,160},{160,192},{192,224},{1,3... | collective-permute-start | bytes 12296 | tf_op jit(solution)/shard_map/ppermute | solution.py:20
  165.5 1.9 %collective-permute-start.25 = (f32[1,1,8,128]{3,2,1,0:T(8,128)S(1)}, f32[1,1,8,128]{3,2,1,0:T(8,128)S(1)}, u32[]{:S(2)}, u32[]{:S(2)}) collective-permute-start(f32[1,1,8,128]{3,2,1,0:T(8,128)S(1)} %get-tuple-element.55), channel_id=1, source_target_pairs={{32,0},{64,32},{96,64},{128,96},{160,128},{192,160},{224,192},{33,... | collective-permute-start | bytes 12296 | tf_op jit(solution)/shard_map/ppermute | solution.py:21
  167.4 3.0 %collective-permute-done.25 = f32[1,1,8,128]{3,2,1,0:T(8,128)S(1)} collective-permute-done((f32[1,1,8,128]{3,2,1,0:T(8,128)S(1)}, f32[1,1,8,128]{3,2,1,0:T(8,128)S(1)}, u32[]{:S(2)}, u32[]{:S(2)}) %collective-permute-start.25) | collective-permute-done | bytes 4128 | tf_op jit(solution)/shard_map/ppermute | solution.py:21
  170.4 2.5 %collective-permute-start.26 = (f32[3,1,8,128]{3,2,1,0:T(8,128)S(1)}, f32[3,1,8,128]{3,2,1,0:T(8,128)S(1)}, u32[]{:S(2)}, u32[]{:S(2)}) collective-permute-start(f32[3,1,8,128]{3,2,1,0:T(8,128)S(1)} %pad_maximum_fusion.9), channel_id=1, source_target_pairs={{0,1},{1,2},{2,3},{3,4},{4,5},{5,6},{6,7},{7,8},{8,9},{9,10},{10,1... | collective-permute-start | bytes 36872 | tf_op jit(solution)/shard_map/ppermute | solution.py:20
  173.0 9.7 %collective-permute-start.27 = (f32[3,1,8,128]{3,2,1,0:T(8,128)S(1)}, f32[3,1,8,128]{3,2,1,0:T(8,128)S(1)}, u32[]{:S(2)}, u32[]{:S(2)}) collective-permute-start(f32[3,1,8,128]{3,2,1,0:T(8,128)S(1)} %pad_maximum_fusion.9), channel_id=1, source_target_pairs={{1,0},{2,1},{3,2},{4,3},{5,4},{6,5},{7,6},{8,7},{9,8},{10,9},{11,1... | collective-permute-start | bytes 36872 | tf_op jit(solution)/shard_map/ppermute | solution.py:21
  182.7 0.8 collective-permute-done.27
  183.5 0.2 fusion.22
  183.8 0.9 convolution_bitcast_fusion.1
  (71 shorter events, 1.2 us)
Async XLA Ops:
  0.0 1.4 copy-start
  2.2 64.1 %collective-permute-start.8 = (bf16[1,1,32,1024]{3,2,1,0:T(8,128)(2,1)S(1)}, bf16[1,1,32,1024]{3,2,1,0:T(8,128)(2,1)S(1)}, u32[]{:S(2)}, u32[]{:S(2)}) collective-permute-start(bf16[1,1,32,1024]{3,2,1,0:T(8,128)(2,1)S(1)} %bitcast.65), channel_id=1, source_target_pairs={{0,32},{32,64},{64,96},{96,128},{128,160},{160,192},{192,224},{1,3... | collective-permute-start | bytes 196616 | tf_op jit(solution)/shard_map/ppermute | solution.py:20
  6.3 60.0 %collective-permute-start.9 = (bf16[1,1,32,1024]{3,2,1,0:T(8,128)(2,1)S(1)}, bf16[1,1,32,1024]{3,2,1,0:T(8,128)(2,1)S(1)}, u32[]{:S(2)}, u32[]{:S(2)}) collective-permute-start(bf16[1,1,32,1024]{3,2,1,0:T(8,128)(2,1)S(1)} %bitcast.66), channel_id=1, source_target_pairs={{32,0},{64,32},{96,64},{128,96},{160,128},{192,160},{224,192},{33,... | collective-permute-start | bytes 196616 | tf_op jit(solution)/shard_map/ppermute | solution.py:21
  9.8 14.3 %collective-permute-start.4 = (bf16[1,1,32,2]{2,3,1,0:T(2,128)(2,1)S(1)}, bf16[1,1,32,2]{2,3,1,0:T(2,128)(2,1)S(1)}, u32[]{:S(2)}, u32[]{:S(2)}) collective-permute-start(bf16[1,1,32,2]{2,3,1,0:T(2,128)(2,1)S(1)} %convert_bitcast_fusion), channel_id=1, source_target_pairs={{0,32},{32,64},{64,96},{96,128},{128,160},{160,192},{192,224},{1,3... | collective-permute-start | bytes 392 | tf_op jit(solution)/shard_map/ppermute | solution.py:20
  13.4 10.7 %collective-permute-start.5 = (bf16[1,1,32,2]{2,3,1,0:T(2,128)(2,1)S(1)}, bf16[1,1,32,2]{2,3,1,0:T(2,128)(2,1)S(1)}, u32[]{:S(2)}, u32[]{:S(2)}) collective-permute-start(bf16[1,1,32,2]{2,3,1,0:T(2,128)(2,1)S(1)} %convert_bitcast_fusion), channel_id=1, source_target_pairs={{32,0},{64,32},{96,64},{128,96},{160,128},{192,160},{224,192},{33,... | collective-permute-start | bytes 392 | tf_op jit(solution)/shard_map/ppermute | solution.py:21
  16.9 27.4 %collective-permute-start.12 = (bf16[1,1,32,128]{3,2,1,0:T(8,128)(2,1)S(1)}, bf16[1,1,32,128]{3,2,1,0:T(8,128)(2,1)S(1)}, u32[]{:S(2)}, u32[]{:S(2)}) collective-permute-start(bf16[1,1,32,128]{3,2,1,0:T(8,128)(2,1)S(1)} %bitcast.77), channel_id=1, source_target_pairs={{0,32},{32,64},{64,96},{96,128},{128,160},{160,192},{192,224},{1,3... | collective-permute-start | bytes 24584 | tf_op jit(solution)/shard_map/ppermute | solution.py:20
  22.3 56.3 %copy-start.1 = (bf16[32,32,128]{2,1,0:T(8,128)(2,1)S(1)}, bf16[32,32,128]{2,1,0:T(8,128)(2,1)}, u32[]{:S(2)}) copy-start(bf16[32,32,128]{2,1,0:T(8,128)(2,1)} %param.14) | copy-start | bytes 786436
  24.1 12.9 %collective-permute-start.6 = (bf16[3,1,32,2]{2,3,1,0:T(2,128)(2,1)S(1)}, bf16[3,1,32,2]{2,3,1,0:T(2,128)(2,1)S(1)}, u32[]{:S(2)}, u32[]{:S(2)}) collective-permute-start(bf16[3,1,32,2]{2,3,1,0:T(2,128)(2,1)S(1)} %pad_maximum_fusion.11), channel_id=1, source_target_pairs={{0,1},{1,2},{2,3},{3,4},{4,5},{5,6},{6,7},{7,8},{8,9},{9,10},{10,1... | collective-permute-start | bytes 1160 | tf_op jit(solution)/shard_map/ppermute | solution.py:20
  32.1 8.2 %collective-permute-start.7 = (bf16[3,1,32,2]{2,3,1,0:T(2,128)(2,1)S(1)}, bf16[3,1,32,2]{2,3,1,0:T(2,128)(2,1)S(1)}, u32[]{:S(2)}, u32[]{:S(2)}) collective-permute-start(bf16[3,1,32,2]{2,3,1,0:T(2,128)(2,1)S(1)} %pad_maximum_fusion.11), channel_id=1, source_target_pairs={{1,0},{2,1},{3,2},{4,3},{5,4},{6,5},{7,6},{8,7},{9,8},{10,9},{11,1... | collective-permute-start | bytes 1160 | tf_op jit(solution)/shard_map/ppermute | solution.py:21
  37.0 7.3 %collective-permute-start.13 = (bf16[1,1,32,128]{3,2,1,0:T(8,128)(2,1)S(1)}, bf16[1,1,32,128]{3,2,1,0:T(8,128)(2,1)S(1)}, u32[]{:S(2)}, u32[]{:S(2)}) collective-permute-start(bf16[1,1,32,128]{3,2,1,0:T(8,128)(2,1)S(1)} %bitcast.78), channel_id=1, source_target_pairs={{32,0},{64,32},{96,64},{128,96},{160,128},{192,160},{224,192},{33,... | collective-permute-start | bytes 24584 | tf_op jit(solution)/shard_map/ppermute | solution.py:21
  40.3 38.3 %collective-permute-start = (bf16[16,32,128]{2,1,0:T(8,128)(2,1)S(1)}, bf16[16,32,128]{2,1,0:T(8,128)(2,1)S(1)}, u32[]{:S(2)}, u32[]{:S(2)}) collective-permute-start(bf16[16,32,128]{2,1,0:T(8,128)(2,1)S(1)} %get-tuple-element.64), channel_id=1, source_target_pairs={{0,32},{32,64},{64,96},{96,128},{128,160},{160,192},{192,224},{1,3... | collective-permute-start | bytes 393224 | tf_op jit(solution)/shard_map/ppermute | solution.py:20
  44.3 19.4 %collective-permute-start.14 = (bf16[3,1,32,128]{3,2,1,0:T(8,128)(2,1)S(1)}, bf16[3,1,32,128]{3,2,1,0:T(8,128)(2,1)S(1)}, u32[]{:S(2)}, u32[]{:S(2)}) collective-permute-start(bf16[3,1,32,128]{3,2,1,0:T(8,128)(2,1)S(1)} %pad_maximum_fusion.6), channel_id=1, source_target_pairs={{0,1},{1,2},{2,3},{3,4},{4,5},{5,6},{6,7},{7,8},{8,9},{9,10},{10,1... | collective-permute-start | bytes 73736 | tf_op jit(solution)/shard_map/ppermute | solution.py:20
  47.9 17.8 %collective-permute-start.15 = (bf16[3,1,32,128]{3,2,1,0:T(8,128)(2,1)S(1)}, bf16[3,1,32,128]{3,2,1,0:T(8,128)(2,1)S(1)}, u32[]{:S(2)}, u32[]{:S(2)}) collective-permute-start(bf16[3,1,32,128]{3,2,1,0:T(8,128)(2,1)S(1)} %pad_maximum_fusion.6), channel_id=1, source_target_pairs={{1,0},{2,1},{3,2},{4,3},{5,4},{6,5},{7,6},{8,7},{9,8},{10,9},{11,1... | collective-permute-start | bytes 73736 | tf_op jit(solution)/shard_map/ppermute | solution.py:21
  63.7 14.9 %collective-permute-start.1 = (bf16[16,32,128]{2,1,0:T(8,128)(2,1)S(1)}, bf16[16,32,128]{2,1,0:T(8,128)(2,1)S(1)}, u32[]{:S(2)}, u32[]{:S(2)}) collective-permute-start(bf16[16,32,128]{2,1,0:T(8,128)(2,1)S(1)} %get-tuple-element.63), channel_id=1, source_target_pairs={{32,0},{64,32},{96,64},{128,96},{160,128},{192,160},{224,192},{33,... | collective-permute-start | bytes 393224 | tf_op jit(solution)/shard_map/ppermute | solution.py:21
  66.4 25.5 %collective-permute-start.10 = (bf16[3,1,32,1024]{3,2,1,0:T(8,128)(2,1)S(1)}, bf16[3,1,32,1024]{3,2,1,0:T(8,128)(2,1)S(1)}, u32[]{:S(2)}, u32[]{:S(2)}) collective-permute-start(bf16[3,1,32,1024]{3,2,1,0:T(8,128)(2,1)S(1)} %pad_maximum_fusion.1), channel_id=1, source_target_pairs={{0,1},{1,2},{2,3},{3,4},{4,5},{5,6},{6,7},{7,8},{8,9},{9,10},{10,1... | collective-permute-start | bytes 589832 | tf_op jit(solution)/shard_map/ppermute | solution.py:20
  68.3 23.6 %collective-permute-start.11 = (bf16[3,1,32,1024]{3,2,1,0:T(8,128)(2,1)S(1)}, bf16[3,1,32,1024]{3,2,1,0:T(8,128)(2,1)S(1)}, u32[]{:S(2)}, u32[]{:S(2)}) collective-permute-start(bf16[3,1,32,1024]{3,2,1,0:T(8,128)(2,1)S(1)} %pad_maximum_fusion.1), channel_id=1, source_target_pairs={{1,0},{2,1},{3,2},{4,3},{5,4},{6,5},{7,6},{8,7},{9,8},{10,9},{11,1... | collective-permute-start | bytes 589832 | tf_op jit(solution)/shard_map/ppermute | solution.py:21
  79.5 27.3 %collective-permute-start.2 = (bf16[64,16,128]{2,1,0:T(8,128)(2,1)}, bf16[64,16,128]{2,1,0:T(8,128)(2,1)}, u32[]{:S(2)}, u32[]{:S(2)}) collective-permute-start(bf16[64,16,128]{2,1,0:T(8,128)(2,1)} %get-tuple-element.61), channel_id=1, source_target_pairs={{0,1},{1,2},{2,3},{3,4},{4,5},{5,6},{6,7},{7,8},{8,9},{9,10},{10,1... | collective-permute-start | bytes 786440 | tf_op jit(solution)/shard_map/ppermute | solution.py:20
  81.4 31.3 %collective-permute-start.3 = (bf16[64,16,128]{2,1,0:T(8,128)(2,1)}, bf16[64,16,128]{2,1,0:T(8,128)(2,1)}, u32[]{:S(2)}, u32[]{:S(2)}) collective-permute-start(bf16[64,16,128]{2,1,0:T(8,128)(2,1)} %get-tuple-element.62), channel_id=1, source_target_pairs={{1,0},{2,1},{3,2},{4,3},{5,4},{6,5},{7,6},{8,7},{9,8},{10,9},{11,1... | collective-permute-start | bytes 786440 | tf_op jit(solution)/shard_map/ppermute | solution.py:21
  93.8 6.6 %copy-start.6 = (bf16[32,64,64]{2,1,0:T(8,128)(2,1)S(1)}, bf16[32,64,64]{2,1,0:T(8,128)(2,1)}, u32[]{:S(2)}) copy-start(bf16[32,64,64]{2,1,0:T(8,128)(2,1)} %convolution_convert_fusion) | copy-start | bytes 786436
  100.4 6.2 %copy-start.4 = (s32[1,1,32]{2,1,0:T(1,128)S(1)}, s32[1,1,32]{2,1,0:T(1,128)}, u32[]{:S(2)}) copy-start(s32[1,1,32]{2,1,0:T(1,128)} %param.19) | copy-start | bytes 388
  100.4 6.3 %copy-start.2 = (bf16[3,3,32,128]{3,2,1,0:T(8,128)(2,1)S(1)}, bf16[3,3,32,128]{3,2,1,0:T(8,128)(2,1)}, u32[]{:S(2)}) copy-start(bf16[3,3,32,128]{3,2,1,0:T(8,128)(2,1)} %pad_maximum_fusion.2) | copy-start | bytes 221188
  105.6 8.9 %copy-start.3 = (f32[32,128]{1,0:T(8,128)S(1)}, f32[32,128]{1,0:T(8,128)}, u32[]{:S(2)}) copy-start(f32[32,128]{1,0:T(8,128)} %get-tuple-element.75) | copy-start | bytes 49156
  105.6 8.9 %copy-start.5 = (pred[8]{0:T(512)(128)(4,1)S(1)}, pred[8]{0:T(512)(128)(4,1)}, u32[]{:S(2)}) copy-start(pred[8]{0:T(512)(128)(4,1)} %get-tuple-element.70) | copy-start | bytes 28
  114.6 5.3 %collective-permute-start.16 = (f32[1,1,8,128]{3,2,1,0:T(8,128)S(1)}, f32[1,1,8,128]{3,2,1,0:T(8,128)S(1)}, u32[]{:S(2)}, u32[]{:S(2)}) collective-permute-start(f32[1,1,8,128]{3,2,1,0:T(8,128)S(1)} %get-tuple-element.59), channel_id=1, source_target_pairs={{0,32},{32,64},{64,96},{96,128},{128,160},{160,192},{192,224},{1,3... | collective-permute-start | bytes 12296 | tf_op jit(solution)/shard_map/ppermute | solution.py:20
  118.0 4.9 %collective-permute-start.17 = (f32[1,1,8,128]{3,2,1,0:T(8,128)S(1)}, f32[1,1,8,128]{3,2,1,0:T(8,128)S(1)}, u32[]{:S(2)}, u32[]{:S(2)}) collective-permute-start(f32[1,1,8,128]{3,2,1,0:T(8,128)S(1)} %get-tuple-element.59), channel_id=1, source_target_pairs={{32,0},{64,32},{96,64},{128,96},{160,128},{192,160},{224,192},{33,... | collective-permute-start | bytes 12296 | tf_op jit(solution)/shard_map/ppermute | solution.py:21
  122.9 12.2 %collective-permute-start.18 = (f32[3,1,8,128]{3,2,1,0:T(8,128)S(1)}, f32[3,1,8,128]{3,2,1,0:T(8,128)S(1)}, u32[]{:S(2)}, u32[]{:S(2)}) collective-permute-start(f32[3,1,8,128]{3,2,1,0:T(8,128)S(1)} %pad_maximum_fusion.7), channel_id=1, source_target_pairs={{0,1},{1,2},{2,3},{3,4},{4,5},{5,6},{6,7},{7,8},{8,9},{9,10},{10,1... | collective-permute-start | bytes 36872 | tf_op jit(solution)/shard_map/ppermute | solution.py:20
  127.0 9.7 %collective-permute-start.19 = (f32[3,1,8,128]{3,2,1,0:T(8,128)S(1)}, f32[3,1,8,128]{3,2,1,0:T(8,128)S(1)}, u32[]{:S(2)}, u32[]{:S(2)}) collective-permute-start(f32[3,1,8,128]{3,2,1,0:T(8,128)S(1)} %pad_maximum_fusion.7), channel_id=1, source_target_pairs={{1,0},{2,1},{3,2},{4,3},{5,4},{6,5},{7,6},{8,7},{9,8},{10,9},{11,1... | collective-permute-start | bytes 36872 | tf_op jit(solution)/shard_map/ppermute | solution.py:21
  137.0 5.0 %collective-permute-start.20 = (f32[1,1,8,128]{3,2,1,0:T(8,128)S(1)}, f32[1,1,8,128]{3,2,1,0:T(8,128)S(1)}, u32[]{:S(2)}, u32[]{:S(2)}) collective-permute-start(f32[1,1,8,128]{3,2,1,0:T(8,128)S(1)} %get-tuple-element.57), channel_id=1, source_target_pairs={{0,32},{32,64},{64,96},{96,128},{128,160},{160,192},{192,224},{1,3... | collective-permute-start | bytes 12296 | tf_op jit(solution)/shard_map/ppermute | solution.py:20
  140.1 4.9 %collective-permute-start.21 = (f32[1,1,8,128]{3,2,1,0:T(8,128)S(1)}, f32[1,1,8,128]{3,2,1,0:T(8,128)S(1)}, u32[]{:S(2)}, u32[]{:S(2)}) collective-permute-start(f32[1,1,8,128]{3,2,1,0:T(8,128)S(1)} %get-tuple-element.57), channel_id=1, source_target_pairs={{32,0},{64,32},{96,64},{128,96},{160,128},{192,160},{224,192},{33,... | collective-permute-start | bytes 12296 | tf_op jit(solution)/shard_map/ppermute | solution.py:21
  145.0 12.2 %collective-permute-start.22 = (f32[3,1,8,128]{3,2,1,0:T(8,128)S(1)}, f32[3,1,8,128]{3,2,1,0:T(8,128)S(1)}, u32[]{:S(2)}, u32[]{:S(2)}) collective-permute-start(f32[3,1,8,128]{3,2,1,0:T(8,128)S(1)} %pad_maximum_fusion.8), channel_id=1, source_target_pairs={{0,1},{1,2},{2,3},{3,4},{4,5},{5,6},{6,7},{7,8},{8,9},{9,10},{10,1... | collective-permute-start | bytes 36872 | tf_op jit(solution)/shard_map/ppermute | solution.py:20
  153.5 8.3 %collective-permute-start.23 = (f32[3,1,8,128]{3,2,1,0:T(8,128)S(1)}, f32[3,1,8,128]{3,2,1,0:T(8,128)S(1)}, u32[]{:S(2)}, u32[]{:S(2)}) collective-permute-start(f32[3,1,8,128]{3,2,1,0:T(8,128)S(1)} %pad_maximum_fusion.8), channel_id=1, source_target_pairs={{1,0},{2,1},{3,2},{4,3},{5,4},{6,5},{7,6},{8,7},{9,8},{10,9},{11,1... | collective-permute-start | bytes 36872 | tf_op jit(solution)/shard_map/ppermute | solution.py:21
  162.1 5.3 %collective-permute-start.24 = (f32[1,1,8,128]{3,2,1,0:T(8,128)S(1)}, f32[1,1,8,128]{3,2,1,0:T(8,128)S(1)}, u32[]{:S(2)}, u32[]{:S(2)}) collective-permute-start(f32[1,1,8,128]{3,2,1,0:T(8,128)S(1)} %get-tuple-element.55), channel_id=1, source_target_pairs={{0,32},{32,64},{64,96},{96,128},{128,160},{160,192},{192,224},{1,3... | collective-permute-start | bytes 12296 | tf_op jit(solution)/shard_map/ppermute | solution.py:20
  165.5 4.9 %collective-permute-start.25 = (f32[1,1,8,128]{3,2,1,0:T(8,128)S(1)}, f32[1,1,8,128]{3,2,1,0:T(8,128)S(1)}, u32[]{:S(2)}, u32[]{:S(2)}) collective-permute-start(f32[1,1,8,128]{3,2,1,0:T(8,128)S(1)} %get-tuple-element.55), channel_id=1, source_target_pairs={{32,0},{64,32},{96,64},{128,96},{160,128},{192,160},{224,192},{33,... | collective-permute-start | bytes 12296 | tf_op jit(solution)/shard_map/ppermute | solution.py:21
  170.4 12.2 %collective-permute-start.26 = (f32[3,1,8,128]{3,2,1,0:T(8,128)S(1)}, f32[3,1,8,128]{3,2,1,0:T(8,128)S(1)}, u32[]{:S(2)}, u32[]{:S(2)}) collective-permute-start(f32[3,1,8,128]{3,2,1,0:T(8,128)S(1)} %pad_maximum_fusion.9), channel_id=1, source_target_pairs={{0,1},{1,2},{2,3},{3,4},{4,5},{5,6},{6,7},{7,8},{8,9},{9,10},{10,1... | collective-permute-start | bytes 36872 | tf_op jit(solution)/shard_map/ppermute | solution.py:20
  173.0 10.5 %collective-permute-start.27 = (f32[3,1,8,128]{3,2,1,0:T(8,128)S(1)}, f32[3,1,8,128]{3,2,1,0:T(8,128)S(1)}, u32[]{:S(2)}, u32[]{:S(2)}) collective-permute-start(f32[3,1,8,128]{3,2,1,0:T(8,128)S(1)} %pad_maximum_fusion.9), channel_id=1, source_target_pairs={{1,0},{2,1},{3,2},{4,3},{5,4},{6,5},{7,6},{8,7},{9,8},{10,9},{11,1... | collective-permute-start | bytes 36872 | tf_op jit(solution)/shard_map/ppermute | solution.py:21
where the time goes:
time: 186 us; the launch traced here: 185 us
  starting transfers between devices  124 us (67%)
  waiting for transfers between devices  23.1 us (12%)
  matrix products  19.4 us (10%)
  local copies, waits for them, and re-layouts  12.3 us (7%)
  other arithmetic  4.62 us (2%)
    ppermute x14, starting transfers between devices, extended(): after = lax.ppermute(first, axis, down)  69 us
    ppermute x14, starting transfers between devices, extended(): before = lax.ppermute(last, axis, up)  54.8 us
    ppermute x14, waiting for transfers between devices, extended(): after = lax.ppermute(first, axis, down)  23.1 us
    dot_general x2, matrix products, paint(): jnp.einsum('kyj,kxj->kyx', spread, cols_hot, preferred_element_type=jnp.f...  8.35 us
    eq x1, local copies, waits for them, and re-layouts, placement(): return (across == anchors[:, None, None] + inside).astype(jnp.bfloat16)  6.43 us
    dot_general x1, matrix products, body(): lax.dot_general(own_canvas, near_canvas, (((1,), (1,)), ((), ())), prefer...  5.24 us
  transfers between devices with their start and end apart: 28, of which 8 were waited for; matrix products, arithmetic and copies ran while one was open for 17% of the time, Pallas kernels for 0%

commit v1 on v0

v1 whole, which is shorter than its diff:
```python
import jax
import jax.numpy as jnp
from jax import lax
from jax.experimental import pallas as pl
from jax.experimental.pallas import tpu as pltpu
from jax.sharding import PartitionSpec as P

K = 32
F = 128
SIDE = 32
PIX = SIDE * SIDE
HALF = SIDE // 2
ROWS = 8
BLOCKS = 4
CHUNK = 16
MESH = pl.DeviceIdType.MESH
AROUND = [(u - 1, v - 1) for u in range(3) for v in range(3)]
f32, bf16, i32 = jnp.float32, jnp.bfloat16, jnp.int32
UP, DOWN, LEFT, RIGHT = (-1, 0), (1, 0), (0, -1), (0, 1)


def flip(o):
    return (-o[0], -o[1])


def slot_of(o):
    return (o[0] + 1) * 3 + o[1] + 1


def nt(x, y):
    return lax.dot_general(x, y, (((1,), (1,)), ((), ())), preferred_element_type=f32)


def nn(x, y):
    return jnp.dot(x, y, preferred_element_type=f32)


def exact(x, y):
    return jnp.dot(x, y, precision=lax.Precision.HIGHEST, preferred_element_type=f32)


def positive(x):
    return jnp.maximum(x, jnp.zeros_like(x))


def kernel(
    movie, foot_in, centres_in, traces_in, counts_in, order_in, out,
    foot, centres, traces, counts, order,
    top_movie, bottom_movie, to_left, to_right, to_up, to_down,
    from_right, from_left, from_down, from_up,
    start, start_up, start_down,
    sum_left, sum_right, sum_from_right, sum_from_left,
    cross_up, cross_down, cross_from_down, cross_from_up,
    change, changes,
    local_sem, send_sem, recv_sem,
):
    a, b = lax.axis_index("ty"), lax.axis_index("tx")
    n_ty, n_tx = lax.axis_size("ty"), lax.axis_size("tx")

    def there(o):
        row, col = a + o[0], b + o[1]
        return (row >= 0) & (row < n_ty) & (col >= 0) & (col < n_tx)

    barrier = pltpu.get_barrier_semaphore()
    expected = jnp.int32(0)
    for o in AROUND:
        if o == (0, 0):
            continue
        present = there(o)

        @pl.when(present)
        def _(o=o):
            pl.semaphore_signal(
                barrier, inc=1, device_id=(a + o[0], b + o[1]), device_id_type=MESH
            )

        expected = expected + present.astype(i32)

    local = []
    for source, target in (
        (order_in, order), (counts_in, counts), (centres_in, centres), (foot_in, foot),
        (traces_in, traces), (movie.at[pl.ds(0, HALF)], top_movie.at[pl.ds(0, HALF)]),
        (movie.at[pl.ds(HALF, HALF)], bottom_movie.at[pl.ds(HALF, HALF)]),
    ):
        copy = pltpu.make_async_copy(source, target, local_sem.at[len(local)])
        copy.start()
        local.append(copy)

    sent = []

    class Remote:
        def __init__(self, source, target, o):
            self.o = o
            index = len(sent)
            self.copy = pltpu.make_async_remote_copy(
                src_ref=source, dst_ref=target,
                send_sem=send_sem.at[index], recv_sem=recv_sem.at[index],
                device_id=(a + o[0], b + o[1]), device_id_type=MESH,
            )
            sent.append(self)

        def start(self):
            pl.when(there(self.o))(self.copy.start)
            return self

        def arrived(self):
            pl.when(there(flip(self.o)))(self.copy.wait_recv)

        def left(self):
            pl.when(there(self.o))(self.copy.wait_send)

    def clear(o, *refs):
        @pl.when(jnp.logical_not(there(o)))
        def _():
            for ref in refs:
                ref[...] = jnp.zeros_like(ref)

    clear(UP, from_up, start_up, cross_from_up, top_movie.at[pl.ds(HALF, HALF)])
    clear(DOWN, from_down, start_down, cross_from_down, bottom_movie.at[pl.ds(0, HALF)])
    clear(LEFT, from_left, sum_from_left)
    clear(RIGHT, from_right, sum_from_right)
    for o in AROUND:
        if o != (0, 0):
            clear(o, *[changes.at[q, slot_of(o)] for q in range(BLOCKS - 1)])

    for copy in local[:3]:
        copy.wait()
    sub = lax.broadcasted_iota(i32, (K, K), 0)
    lane = lax.broadcasted_iota(i32, (K, K), 1)
    order_row = order[0:1, :]
    alive_row = order_row < counts[0:1, 0:1]
    eye = sub == lane
    order_col = jnp.sum(
        jnp.where(eye, jnp.broadcast_to(order_row, (K, K)), 0).astype(f32), axis=1, keepdims=True
    ).astype(i32)
    alive_col = order_col < counts[0:1, 0:1]
    chooser = jnp.where((lane == order_col) & alive_col, 1.0, 0.0)
    back = jnp.where(sub == order_row, 1.0, 0.0)
    places = exact(chooser, centres[...].astype(f32)).astype(i32)
    row_at, col_at = places[:, 0:1], places[:, 1:2]
    for copy in local[3:5]:
        copy.wait()
    chooser16 = chooser.astype(bf16)
    ordered = nn(chooser16, foot[...])
    start_value = nn(chooser16, traces[...])
    start[...] = start_value.astype(bf16)

    lanes = lax.broadcasted_iota(i32, (K, F), 1)
    group, across = lanes >> 5, lanes & 31
    turn, shift = (row_at + HALF) & 31, (col_at + HALF) & 31
    fine, coarse = turn & 3, turn >> 2
    index = (((group - fine) & 3) << 5) + ((across - shift) & 31)
    slabs = [
        jnp.take_along_axis(ordered[:, v * F:(v + 1) * F], index, axis=1) for v in range(8)
    ]
    carry = group < fine
    slabs = [jnp.where(carry, slabs[(v - 1) % 8], slabs[v]) for v in range(8)]
    for bit in (1, 2, 4):
        taken = jnp.broadcast_to((coarse & bit) != 0, (K, F))
        slabs = [jnp.where(taken, slabs[(v - bit) % 8], slabs[v]) for v in range(8)]
    left_half = ((across + HALF) & 31) >= col_at
    for v in range(8):
        upper = ((4 * v + group + HALF) & 31) >= row_at
        x = slabs[v]
        by_row = jnp.where(upper, x, -x)
        by_col = jnp.where(left_half, x, -x)
        here = pl.ds(v * F, F)
        to_left[:, here] = jnp.where(left_half, by_row, 0.0).astype(bf16)
        to_right[:, here] = jnp.where(left_half, 0.0, by_row).astype(bf16)
        to_up[:, here] = jnp.where(upper, by_col, 0.0).astype(bf16)
        to_down[:, here] = jnp.where(upper, 0.0, by_col).astype(bf16)
    for copy in local[5:]:
        copy.wait()

    pl.semaphore_wait(barrier, expected)

    def part(ref, c):
        return ref.at[pl.ds(c * CHUNK, CHUNK)]

    side = [
        [Remote(part(to_left, c), part(from_right, c), LEFT),
         Remote(part(to_right, c), part(from_left, c), RIGHT)]
        for c in range(2)
    ]
    vertical = [
        Remote(to_up, from_down, UP), Remote(to_down, from_up, DOWN),
        Remote(start, start_down, UP), Remote(start, start_up, DOWN),
        Remote(top_movie.at[pl.ds(0, HALF)], bottom_movie.at[pl.ds(0, HALF)], UP),
        Remote(bottom_movie.at[pl.ds(HALF, HALF)], top_movie.at[pl.ds(HALF, HALF)], DOWN),
    ]
    for message in side[0] + vertical + side[1]:
        message.start()

    own_tl, own_bl = positive(to_left[...]), positive(-to_left[...])
    own_tr, own_br = positive(to_right[...]), positive(-to_right[...])
    pixel = lax.broadcasted_iota(i32, (K, PIX), 1) & 31
    near_side = jnp.where(pixel < HALF, 1.0, 0.0).astype(bf16)
    far_side = jnp.where(pixel < HALF, 0.0, 1.0).astype(bf16)
    for message in vertical:
        message.arrived()
    up_bl, up_br = positive(from_up[...]), positive(-from_up[...])
    down_tl, down_tr = positive(from_down[...]), positive(-from_down[...])
    above = top_movie[...].reshape(PIX, F)
    below = bottom_movie[...].reshape(PIX, F)
    s_own, s_up, s_down = (x[...].astype(f32) for x in (start, start_up, start_down))
    column_top = jnp.concatenate([s_own, s_up], axis=0)
    column_bottom = jnp.concatenate([s_own, s_down], axis=0)
    stack_tl = jnp.concatenate([own_tl, up_bl], axis=0)
    stack_tr = jnp.concatenate([own_tr, up_br], axis=0)
    stack_bl = jnp.concatenate([own_bl, down_tl], axis=0)
    stack_br = jnp.concatenate([own_br, down_tr], axis=0)

    own_top = nt(stack_tl, own_tl) + nt(stack_tr, own_tr)
    own_bottom = nt(stack_bl, own_bl) + nt(stack_br, own_br)
    own_own = own_top[:K] + own_bottom[:K]
    own_up, own_down = own_top[K:], own_bottom[K:]
    strip_top = own_tl * near_side + own_tr * far_side
    strip_bottom = own_bl * near_side + own_br * far_side
    total = nn(strip_top, above) + nn(strip_bottom, below)
    column = jnp.concatenate([own_own, own_up, own_down], axis=0)
    total = total - exact(column.T, jnp.concatenate([s_own, s_up, s_down], axis=0))
    diagonal = jnp.sum(jnp.where(eye, own_own, 0.0), axis=1, keepdims=True)
    divisor = jnp.where(alive_col, diagonal, 1.0)

    returns, grams = [], []
    for c in range(2):
        for message in side[c]:
            message.arrived()
        from_l, from_r = part(from_left, c)[...], part(from_right, c)[...]
        l_tr, l_br = positive(from_l), positive(-from_l)
        r_tl, r_bl = positive(from_r), positive(-from_r)
        gram_tl, gram_bl = nt(l_tr, stack_tl), nt(l_br, stack_bl)
        gram_tr, gram_br = nt(r_tl, stack_tr), nt(r_bl, stack_br)
        grams.append((gram_tl, gram_bl, gram_tr, gram_br))
        near, far = near_side[:CHUNK], far_side[:CHUNK]
        upper = jnp.concatenate([l_tr * near, r_tl * far], axis=0)
        lower = jnp.concatenate([l_br * near, r_bl * far], axis=0)
        both = nn(upper, above) + nn(lower, below)
        both = both - exact(jnp.concatenate([gram_tl, gram_tr], axis=0), column_top)
        both = both - exact(jnp.concatenate([gram_bl, gram_br], axis=0), column_bottom)
        part(sum_left, c)[...] = both[:CHUNK]
        part(sum_right, c)[...] = both[CHUNK:]
        pair = [
            Remote(part(sum_left, c), part(sum_from_right, c), LEFT).start(),
            Remote(part(sum_right, c), part(sum_from_left, c), RIGHT).start(),
        ]
        returns.append(pair)
    gram_tl, gram_bl, gram_tr, gram_br = (jnp.concatenate(g, axis=0) for g in zip(*grams))
    cross_up[...] = jnp.concatenate([gram_tl[:, K:], gram_tr[:, K:]], axis=0)
    cross_down[...] = jnp.concatenate([gram_bl[:, K:], gram_br[:, K:]], axis=0)
    crossing = [
        Remote(cross_up, cross_from_down, UP).start(),
        Remote(cross_down, cross_from_up, DOWN).start(),
    ]
    own_left = gram_tl[:, :K] + gram_bl[:, :K]
    own_right = gram_tr[:, :K] + gram_br[:, :K]
    for message in crossing:
        message.arrived()
    around = [
        cross_from_up[:K, :], own_up, cross_from_up[K:, :],
        own_left, own_own, own_right,
        cross_from_down[:K, :], own_down, cross_from_down[K:, :],
    ]
    columns = [
        jnp.concatenate([m[q * ROWS:(q + 1) * ROWS] for m in around], axis=0).T
        for q in range(BLOCKS - 1)
    ]

    current = []
    for q in range(BLOCKS):
        if q % 2 == 0:
            for message in returns[q // 2]:
                message.arrived()
        rows = slice(q * ROWS, (q + 1) * ROWS)
        if q % 2 == 0:
            pair_rows = slice(q * ROWS, (q + 2) * ROWS)
            gathered = sum_from_left[pair_rows, :] + sum_from_right[pair_rows, :]
            total = jnp.concatenate(
                [total[:q * ROWS]] * (q > 0)
                + [total[pair_rows] + gathered]
                + [total[(q + 2) * ROWS:]] * (q + 2 < BLOCKS),
                axis=0,
            )
        previous = start_value[rows]
        renewed = jnp.maximum(previous + total[rows] / divisor[rows], 0.0)
        renewed = jnp.where(alive_col[rows], renewed, 0.0)
        current.append(renewed)
        if q + 1 == BLOCKS:
            break
        mine = renewed - previous
        change[q] = mine
        messages = [
            Remote(change.at[q], changes.at[q, slot_of(flip(o))], o).start()
            for o in AROUND if o != (0, 0)
        ]
        for message in messages:
            message.arrived()
        moved = jnp.concatenate(
            [mine if n == 4 else changes[q, n] for n in range(9)], axis=0
        )
        total = total - exact(columns[q], moved)
    out[...] = exact(back, jnp.concatenate(current, axis=0))
    for message in sent:
        message.left()


def body(movie, footprints, centres, traces, counts, order):
    messages = 4 + 6 + 4 + 2 + 8 * (BLOCKS - 1)
    any_space = pl.BlockSpec(memory_space=pl.ANY)
    result = pl.pallas_call(
        kernel,
        name="hals",
        out_shape=jax.ShapeDtypeStruct((K, F), f32),
        in_specs=[any_space] * 6,
        out_specs=pl.BlockSpec(memory_space=pltpu.VMEM),
        scratch_shapes=[
            pltpu.VMEM((K, PIX), bf16), pltpu.VMEM((K, 2), i32), pltpu.VMEM((K, F), bf16),
            pltpu.VMEM((1, 1), i32), pltpu.VMEM((1, K), i32),
            pltpu.VMEM((SIDE, SIDE, F), bf16), pltpu.VMEM((SIDE, SIDE, F), bf16),
            *[pltpu.VMEM((K, PIX), bf16) for _ in range(8)],
            *[pltpu.VMEM((K, F), bf16) for _ in range(3)],
            *[pltpu.VMEM((K, F), f32) for _ in range(4)],
            *[pltpu.VMEM((2 * K, K), f32) for _ in range(4)],
            pltpu.VMEM((BLOCKS - 1, ROWS, F), f32), pltpu.VMEM((BLOCKS - 1, 9, ROWS, F), f32),
            pltpu.SemaphoreType.DMA((7,)),
            pltpu.SemaphoreType.DMA((messages,)), pltpu.SemaphoreType.DMA((messages,)),
        ],
        compiler_params=pltpu.CompilerParams(collective_id=0, has_side_effects=True),
    )(movie, footprints[0, 0], centres[0, 0], traces[0, 0], counts, order[0])
    return result[None, None]


def solution(mesh):
    in_specs = (
        P("ty", "tx", None),
        P("ty", "tx", None, None),
        P("ty", "tx", None, None),
        P("ty", "tx", None, None),
        P("ty", "tx"),
        P("ty", "tx", None),
    )
    out_specs = P("ty", "tx", None, None)
    return jax.shard_map(body, mesh=mesh, in_specs=in_specs, out_specs=out_specs, check_vma=False)
```

time: 186 us -> 50.6 us (0.27)
  starting transfers between devices: 124 us -> 0 us
  Pallas kernels: 0 us -> 47 us
  waiting for transfers between devices: 23.1 us -> 0 us
  matrix products: 19.4 us -> 0 us
  local copies, waits for them, and re-layouts: 12.3 us -> 2.69 us
  other arithmetic: 4.62 us -> 0 us
    ppermute x28 -> x0, starting transfers between devices: 124 us -> none  [the longest x14 69 us: extended(): after = lax.ppermute(first, axis, down)]
    pallas_call x0 -> x1, Pallas kernels: none -> 47 us  [body(): pl.pallas_call(kernel, name='hals', out_shape=jax.ShapeDtypeStruct((K, F)...]
    ppermute x28 -> x0, waiting for transfers between devices: 23.1 us -> none  [the longest x14 23.1 us: extended(): after = lax.ppermute(first, axis, down)]
    dot_general x11 -> x0, matrix products: 19.4 us -> none  [the longest x2 8.35 us: paint(): jnp.einsum('kyj,kxj->kyx', spread, cols_hot, preferred_element_type=jnp.f...]
    eq x1 -> x0, local copies, waits for them, and re-layouts: 6.43 us -> none  [placement(): return (across == anchors[:, None, None] + inside).astype(jnp.bfloat16)]
    slice x5 -> x0, local copies, waits for them, and re-layouts: 2.4 us -> none  [the longest x1 0.99 us: extended(): first = lax.slice_in_dim(x, 0, width, axis=dim)]
    reshape x2 -> x0, local copies, waits for them, and re-layouts: 1.99 us -> none  [the longest x1 1.81 us: body(): near_patch = near_flat.reshape(9 * slot_count, PATCH, PATCH)]
  transfers between devices with their start and end apart: 28 -> 0, of which waited for: 8 -> 0; matrix products, arithmetic and copies ran while one was open for 17% -> 0% of each run, Pallas kernels for 0% -> 0%
where the time goes in v1:
time: 50.6 us; the launch traced here: 50.4 us
  Pallas kernels  47 us (93%)
  local copies, waits for them, and re-layouts  2.69 us (5%)
  between operations  0.67 us (1%)
    pallas_call x1, Pallas kernels, body(): pl.pallas_call(kernel, name='hals', out_shape=jax.ShapeDtypeStruct((K, F)...  47 us
    unnamed x3, local copies, waits for them, and re-layouts  2 us

profile of v1, /device:TPU:7, one launch (start us, length us, event | category | flops | bytes accessed | tf_op | source)
XLA Modules:
  0.0 50.4 jit_solution(1180035505063221199)
XLA Ops:
  0.7 0.0 copy-start
  0.7 0.7 %copy-done = s32[1,1,32,2]{2,3,1,0:T(2,128)S(1)} copy-done((s32[1,1,32,2]{2,3,1,0:T(2,128)S(1)}, s32[1,1,32,2]{2,3,1,0:T(2,128)}, u32[]{:S(2)}) %copy-start) | copy-done | bytes 280
  1.3 0.7 %copy.7.centres_in = s32[32,2]{1,0:T(8,128)} copy(s32[32,2]{0,1:T(2,128)S(1)} %bitcast.8) | data formatting | bytes 512 | tf_op jit(solution)/shard_map/squeeze | solution.py:329
  2.0 47.0 %hals.1 = f32[32,128]{1,0:T(8,128)} custom-call(bf16[32,32,128]{2,1,0:T(8,128)(2,1)} %movie.1, bf16[32,1024]{1,0:T(8,128)(2,1)} %bitcast.6, s32[32,2]{1,0:T(8,128)} %copy.7.centres_in, bf16[32,128]{1,0:T(8,128)(2,1)} %bitcast.7, s32[1,1]{1,0:T(1,128)S(6)} %copy.9.counts_in, s32[1,32]{1,0:T(1,128)} %bitcast.9), custom_call_target="tpu_custom_call" | custom-call | tf_op jit(solution)/shard_map/hals/pallas_call | solution.py:310
  49.0 1.3 %copy.10 = f32[1,1,32,128]{3,2,1,0:T(8,128)} copy(f32[1,1,32,128]{3,2,1,0:T(8,128)} %bitcast.5) | data formatting | bytes 32768
Async XLA Ops:
  0.7 0.7 %copy-start = (s32[1,1,32,2]{2,3,1,0:T(2,128)S(1)}, s32[1,1,32,2]{2,3,1,0:T(2,128)}, u32[]{:S(2)}) copy-start(s32[1,1,32,2]{2,3,1,0:T(2,128)} %param.8) | copy-start | bytes 772

commit v2 on v1

v2 whole, which is shorter than its diff:
```python
import jax
import jax.numpy as jnp
from jax import lax
from jax.experimental import pallas as pl
from jax.experimental.pallas import tpu as pltpu
from jax.sharding import PartitionSpec as P

K = 32
F = 128
SIDE = 32
PIX = SIDE * SIDE
HALF = SIDE // 2
ROWS = 8
BLOCKS = 4
FIRST = 24
MESH = pl.DeviceIdType.MESH
NEAR = [(u, v) for u in (-1, 0, 1) for v in (-1, 0, 1)]
WIDE = [(u, v) for u in range(-2, 3) for v in range(-2, 3)]
RING = [o for o in WIDE if o not in NEAR]
BAND = [(u, v) for u in (-1, 0, 1) for v in range(-2, 3) if (u, v) != (0, 0)]
HERE = (0, 0)
f32, bf16, i32 = jnp.float32, jnp.bfloat16, jnp.int32
UP, DOWN, LEFT, RIGHT = (-1, 0), (1, 0), (0, -1), (0, 1)


def flip(o):
    return (-o[0], -o[1])


def plus(o, p):
    return (o[0] + p[0], o[1] + p[1])


def nt(x, y):
    return lax.dot_general(x, y, (((1,), (1,)), ((), ())), preferred_element_type=f32)


def tn(x, y):
    return lax.dot_general(x, y, (((0,), (0,)), ((), ())), preferred_element_type=f32)


def nn(x, y):
    return jnp.dot(x, y, preferred_element_type=f32)


def rounded(x):
    return x.astype(bf16).astype(f32)


def lanes_of(x):
    high = rounded(x)
    return jnp.concatenate([high, high, x - high], axis=1).astype(bf16)


def rows_of(x):
    high = rounded(x)
    return jnp.concatenate([high, x - high, high], axis=0).astype(bf16)


def positive(x):
    return jnp.maximum(x, jnp.zeros_like(x))


def kernel(
    movie, foot_in, centres_in, traces_in, counts_in, order_in, out,
    foot, centres, traces, counts, order,
    top_movie, bottom_movie, to_left, to_right, to_up, to_down,
    from_right, from_left, from_down, from_up,
    start, start_up, start_down, info, infos,
    about, abouts, sum_left, sum_right, sum_from_right, sum_from_left,
    cross_up, cross_down, cross_from_down, cross_from_up,
    margin, margins, step, steps, far_steps,
    local_sem, send_sem, recv_sem,
):
    a, b = lax.axis_index("ty"), lax.axis_index("tx")
    n_ty, n_tx = lax.axis_size("ty"), lax.axis_size("tx")

    def there(o):
        row, col = a + o[0], b + o[1]
        return (row >= 0) & (row < n_ty) & (col >= 0) & (col < n_tx)

    barrier = pltpu.get_barrier_semaphore()
    expected = jnp.int32(0)
    for o in WIDE:
        if o == HERE:
            continue
        present = there(o)

        @pl.when(present)
        def _(o=o):
            pl.semaphore_signal(
                barrier, inc=1, device_id=(a + o[0], b + o[1]), device_id_type=MESH
            )

        expected = expected + present.astype(i32)

    local = []
    for source, target in (
        (order_in, order), (counts_in, counts), (centres_in, centres), (foot_in, foot),
        (traces_in, traces), (movie.at[pl.ds(0, HALF)], top_movie.at[pl.ds(0, HALF)]),
        (movie.at[pl.ds(HALF, HALF)], bottom_movie.at[pl.ds(HALF, HALF)]),
    ):
        copy = pltpu.make_async_copy(source, target, local_sem.at[len(local)])
        copy.start()
        local.append(copy)

    sent = []

    class Remote:
        def __init__(self, source, target, o):
            self.o = o
            index = len(sent)
            self.copy = pltpu.make_async_remote_copy(
                src_ref=source, dst_ref=target,
                send_sem=send_sem.at[index], recv_sem=recv_sem.at[index],
                device_id=(a + o[0], b + o[1]), device_id_type=MESH,
            )
            sent.append(self)

        def start(self):
            pl.when(there(self.o))(self.copy.start)
            return self

        def arrived(self):
            pl.when(there(flip(self.o)))(self.copy.wait_recv)

        def left(self):
            pl.when(there(self.o))(self.copy.wait_send)

    def clear(o, *refs):
        @pl.when(jnp.logical_not(there(o)))
        def _():
            for ref in refs:
                ref[...] = jnp.zeros_like(ref)

    def slot(o):
        return (o[0] + 1) * 3 + o[1] + 1

    clear(UP, from_up, start_up, cross_from_up, top_movie.at[pl.ds(HALF, HALF)])
    clear(DOWN, from_down, start_down, cross_from_down, bottom_movie.at[pl.ds(0, HALF)])
    clear(LEFT, from_left, sum_from_left)
    clear(RIGHT, from_right, sum_from_right)
    for o in NEAR:
        if o != HERE:
            clear(o, infos.at[slot(o)], margins.at[slot(o)], steps.at[slot(o)])
    for o in BAND:
        clear(o, abouts.at[o[0] + 1, o[1] + 2])
    for o in RING:
        clear(o, far_steps.at[RING.index(o)])

    for copy in local[:3]:
        copy.wait()
    sub = lax.broadcasted_iota(i32, (K, K), 0)
    lane = lax.broadcasted_iota(i32, (K, K), 1)

    def to_column(row, pick):
        spread = jnp.where(pick, jnp.broadcast_to(row, (K, K)), 0)
        return jnp.sum(spread.astype(f32), axis=1, keepdims=True)

    order_row = order[0:1, :]
    order_col = to_column(order_row, sub == lane).astype(i32)
    alive_col = order_col < counts[0:1, 0:1]
    picked = (lane == order_col) & alive_col
    row_at = to_column(centres[0:1, :], picked).astype(i32)
    col_at = to_column(centres[1:2, :], picked).astype(i32)
    for copy in local[3:5]:
        copy.wait()
    chooser = jnp.where(picked, 1.0, 0.0).astype(bf16)
    ordered = nn(chooser, foot[...])
    start_value = nn(chooser, traces[...])
    start[...] = start_value.astype(bf16)
    diagonal = jnp.sum(ordered * ordered, axis=1, keepdims=True)
    divisor = jnp.where(alive_col, diagonal, 1.0)
    level = jnp.broadcast_to(divisor, (K, F))
    level_high = rounded(level)
    level_mid = rounded(level - level_high)
    level_low = level - level_high - level_mid
    wide_lane = lax.broadcasted_iota(i32, (K, F), 1)
    level_parts = jnp.where(
        wide_lane == 0, level_high, jnp.where(wide_lane == 1, level_mid, level_low)
    )
    info[...] = jnp.concatenate(
        [start_value[:ROWS], start_value[2 * ROWS:3 * ROWS],
         level_parts[:ROWS], level_parts[2 * ROWS:3 * ROWS]], axis=0
    ).astype(bf16)

    group, across = wide_lane >> 5, wide_lane & 31
    turn, shift = (row_at + HALF) & 31, (col_at + HALF) & 31
    fine, coarse = turn & 3, turn >> 2
    index = (((group - fine) & 3) << 5) + ((across - shift) & 31)
    slabs = [
        jnp.take_along_axis(ordered[:, v * F:(v + 1) * F], index, axis=1) for v in range(8)
    ]
    carry = group < fine
    slabs = [jnp.where(carry, slabs[(v - 1) % 8], slabs[v]) for v in range(8)]
    for bit in (1, 2, 4):
        taken = jnp.broadcast_to((coarse & bit) != 0, (K, F))
        slabs = [jnp.where(taken, slabs[(v - bit) % 8], slabs[v]) for v in range(8)]
    left_half = ((across + HALF) & 31) >= col_at
    for v in range(8):
        upper = ((4 * v + group + HALF) & 31) >= row_at
        x = slabs[v]
        by_row = jnp.where(upper, x, -x)
        by_col = jnp.where(left_half, x, -x)
        here = pl.ds(v * F, F)
        to_left[:, here] = jnp.where(left_half, by_row, 0.0).astype(bf16)
        to_right[:, here] = jnp.where(left_half, 0.0, by_row).astype(bf16)
        to_up[:, here] = jnp.where(upper, by_col, 0.0).astype(bf16)
        to_down[:, here] = jnp.where(upper, 0.0, by_col).astype(bf16)
    for copy in local[5:]:
        copy.wait()

    pl.semaphore_wait(barrier, expected)

    early, late = pl.ds(0, FIRST), pl.ds(FIRST, K - FIRST)
    side, side_late = [
        [Remote(to_left.at[rows], from_right.at[rows], LEFT),
         Remote(to_right.at[rows], from_left.at[rows], RIGHT)]
        for rows in (early, late)
    ]
    vertical = [
        Remote(to_up, from_down, UP), Remote(to_down, from_up, DOWN),
        Remote(start, start_down, UP), Remote(start, start_up, DOWN),
        Remote(top_movie.at[pl.ds(0, HALF)], bottom_movie.at[pl.ds(0, HALF)], UP),
        Remote(bottom_movie.at[pl.ds(HALF, HALF)], top_movie.at[pl.ds(HALF, HALF)], DOWN),
    ]
    known = [Remote(info, infos.at[slot(flip(o))], o) for o in NEAR if o != HERE]
    for message in side + vertical + side_late + known:
        message.start()

    own_tl, own_bl = positive(to_left[...]), positive(-to_left[...])
    own_tr, own_br = positive(to_right[...]), positive(-to_right[...])
    for message in vertical:
        message.arrived()
    up_bl, up_br = positive(from_up[...]), positive(-from_up[...])
    down_tl, down_tr = positive(from_down[...]), positive(-from_down[...])
    column_top = jnp.concatenate([start[...], start_up[...]], axis=0)
    column_bottom = jnp.concatenate([start[...], start_down[...]], axis=0)
    stack_tl = jnp.concatenate([own_tl, up_bl], axis=0)
    stack_tr = jnp.concatenate([own_tr, up_br], axis=0)
    stack_bl = jnp.concatenate([own_bl, down_tl], axis=0)
    stack_br = jnp.concatenate([own_br, down_tr], axis=0)

    near_rows = (lax.broadcasted_iota(i32, (PIX, F), 0) & 31) < HALF

    def residual(pixels, near, stack, column):
        seen = pixels[...].reshape(PIX, F).astype(f32)
        seen = jnp.where(near_rows, seen, 0.0) if near else jnp.where(near_rows, 0.0, seen)
        rest = seen - tn(stack, column)
        high = rounded(rest)
        return jnp.concatenate([high, rest - high], axis=1).astype(bf16)

    rest_tl = residual(top_movie, True, stack_tl, column_top)
    rest_tr = residual(top_movie, False, stack_tr, column_top)
    rest_bl = residual(bottom_movie, True, stack_bl, column_bottom)
    rest_br = residual(bottom_movie, False, stack_br, column_bottom)
    both = nn(own_tl, rest_tl) + nn(own_tr, rest_tr) + nn(own_bl, rest_bl) + nn(own_br, rest_br)
    total = both[:, :F] + both[:, F:]

    def halves(rows):
        l, r = from_left[rows, :], from_right[rows, :]
        return positive(l), positive(-l), positive(r), positive(-r)

    def side_sums(l_tr, l_br, r_tl, r_bl):
        l = nn(l_tr, rest_tl) + nn(l_br, rest_bl)
        r = nn(r_tl, rest_tr) + nn(r_bl, rest_br)
        return l[:, :F] + l[:, F:], r[:, :F] + r[:, F:]

    for message in side:
        message.arrived()
    parts = halves(early)
    l_sum, r_sum = side_sums(*parts)
    about[0], about[1], about[2] = l_sum[:ROWS], total[:ROWS], r_sum[:ROWS]
    sum_left[:FIRST, :], sum_right[:FIRST, :] = l_sum, r_sum
    first_sums = []
    for o in BAND:
        low, high = max(0, o[1]), min(3, 3 + o[1])
        first_sums.append(
            Remote(
                about.at[pl.ds(low, high - low)],
                abouts.at[1 - o[0], 2 - o[1], pl.ds(low - o[1], high - low)], o,
            ).start()
        )
    middle = pl.ds(ROWS, FIRST - ROWS)
    returned = [
        Remote(sum_left.at[middle], sum_from_right.at[middle], LEFT).start(),
        Remote(sum_right.at[middle], sum_from_left.at[middle], RIGHT).start(),
    ]

    l_tr, l_br, r_tl, r_bl = parts
    gram_tl, gram_bl = nt(l_tr, stack_tl), nt(l_br, stack_bl)
    gram_tr, gram_br = nt(r_tl, stack_tr), nt(r_bl, stack_br)
    cross_up[...] = jnp.concatenate([gram_tl[:, K:], gram_tr[:, K:]], axis=0)
    cross_down[...] = jnp.concatenate([gram_bl[:, K:], gram_br[:, K:]], axis=0)
    crossing = [
        Remote(cross_up, cross_from_down, UP).start(),
        Remote(cross_down, cross_from_up, DOWN).start(),
    ]
    own_left = gram_tl[:, :K] + gram_bl[:, :K]
    own_right = gram_tr[:, :K] + gram_br[:, :K]
    own_top = nt(stack_tl, own_tl) + nt(stack_tr, own_tr)
    own_bottom = nt(stack_bl, own_bl) + nt(stack_br, own_br)
    own_own = own_top[:K] + own_bottom[:K]
    own_up, own_down = own_top[K:], own_bottom[K:]

    for message in side_late:
        message.arrived()
    l_sum, r_sum = side_sums(*halves(late))
    sum_left[FIRST:, :], sum_right[FIRST:, :] = l_sum, r_sum
    returned_late = [
        Remote(sum_left.at[late], sum_from_right.at[late], LEFT).start(),
        Remote(sum_right.at[late], sum_from_left.at[late], RIGHT).start(),
    ]

    for message in crossing:
        message.arrived()
    around = [
        cross_from_up[:FIRST, :], own_up, cross_from_up[FIRST:, :],
        own_left, own_own, own_right,
        cross_from_down[:FIRST, :], own_down, cross_from_down[FIRST:, :],
    ]
    columns = [
        jnp.concatenate([m[q * ROWS:(q + 1) * ROWS] for m in around], axis=0).T
        for q in range(BLOCKS - 1)
    ]
    margin[...] = columns[1][2 * ROWS:3 * ROWS]
    lent = [Remote(margin, margins.at[slot(flip(o))], o).start() for o in NEAR if o != HERE]
    columns = [lanes_of(x) for x in columns]

    def stepped(previous, left_over, level):
        return jnp.maximum(previous + left_over / level, 0.0)

    def rows(q):
        return slice(q * ROWS, (q + 1) * ROWS)

    for message in known:
        message.arrived()
    facts = {}
    for o in NEAR:
        if o == HERE:
            facts[o] = [start_value[rows(0)], start_value[rows(2)], divisor[rows(0)], divisor[rows(2)]]
            continue
        x = infos[slot(o)].astype(f32)
        level = x[:, 0:1] + x[:, 1:2] + x[:, 2:3]
        levels = (jnp.where(y == 0.0, 1.0, y) for y in (level[rows(2)], level[rows(3)]))
        facts[o] = [x[rows(0)], x[rows(1)], *levels]

    for message in first_sums:
        message.arrived()
    moved = []
    for o in NEAR:
        left_over = None
        for v in range(-2, 3):
            if abs(v - o[1]) > 1:
                continue
            piece = (
                about[o[1] + 1] if (o[0], v) == HERE
                else abouts[o[0] + 1, v + 2, o[1] + 1]
            )
            left_over = piece if left_over is None else left_over + piece
        previous = facts[o][0]
        renewed = stepped(previous, left_over, facts[o][2])
        if o == HERE:
            renewed = jnp.where(alive_col[rows(0)], renewed, 0.0)
            current = [renewed]
        moved.append(renewed - previous)
    for message in returned:
        message.arrived()
    total = total[ROWS:FIRST] + sum_from_left[ROWS:FIRST, :] + sum_from_right[ROWS:FIRST, :]
    change = nn(columns[0][ROWS:], rows_of(jnp.concatenate(moved, axis=0)))
    total = total - change[:FIRST - ROWS]

    previous = start_value[rows(1)]
    renewed = stepped(previous, total[:ROWS], divisor[rows(1)])
    renewed = jnp.where(alive_col[rows(1)], renewed, 0.0)
    current.append(renewed)
    own_step = renewed - previous
    step[:ROWS, :] = own_step
    step[ROWS:, :] = total[ROWS:]
    moves = [
        Remote(step, steps.at[slot(flip(o))], o).start() if o in NEAR
        else Remote(
            step.at[pl.ds(0, ROWS)], far_steps.at[RING.index(flip(o))], o
        ).start()
        for o in WIDE if o != HERE
    ]
    for message in returned_late:
        message.arrived()
    last = both[FIRST:, :F] + both[FIRST:, F:] + sum_from_left[FIRST:, :]
    last = last + sum_from_right[FIRST:, :] - change[FIRST - ROWS:]
    for message in lent:
        message.arrived()
    weights = {
        o: lanes_of(margin[...] if o == HERE else margins[slot(o)]) for o in NEAR
    }

    for message in moves:
        message.arrived()
    taken = {
        o: own_step if o == HERE
        else steps[slot(o), :ROWS, :] if o in NEAR
        else far_steps[RING.index(o)]
        for o in WIDE
    }
    moved = []
    for o in NEAR:
        nearby = rows_of(jnp.concatenate([taken[plus(o, p)] for p in NEAR], axis=0))
        if o == HERE:
            left_over = total[ROWS:]
            last = last - nn(columns[1][FIRST:], nearby)
        else:
            left_over = steps[slot(o), ROWS:, :]
        left_over = left_over - nn(weights[o], nearby)
        previous = facts[o][1]
        renewed = stepped(previous, left_over, facts[o][3])
        if o == HERE:
            renewed = jnp.where(alive_col[rows(2)], renewed, 0.0)
            current.append(renewed)
        moved.append(renewed - previous)

    last = last - nn(columns[2][FIRST:], rows_of(jnp.concatenate(moved, axis=0)))
    renewed = stepped(start_value[rows(3)], last, divisor[rows(3)])
    current.append(jnp.where(alive_col[rows(3)], renewed, 0.0))
    result = jnp.concatenate(current, axis=0)
    high = rounded(result)
    mid = rounded(result - high)
    back = jnp.where(sub == order_row, 1.0, 0.0)
    out[...] = nn(
        jnp.concatenate([back, back, back], axis=1).astype(bf16),
        jnp.concatenate([high, mid, result - high - mid], axis=0).astype(bf16),
    )
    for message in sent:
        message.left()


def body(movie, footprints, centres, traces, counts, order):
    messages = 4 + 6 + 8 + len(BAND) + 4 + 2 + 8 + 24
    any_space = pl.BlockSpec(memory_space=pl.ANY)
    result = pl.pallas_call(
        kernel,
        name="hals",
        out_shape=pltpu.VMEM((K, F), f32),
        in_specs=[any_space] * 6,
        out_specs=pl.BlockSpec(memory_space=pltpu.VMEM),
        scratch_shapes=[
            pltpu.VMEM((K, PIX), bf16), pltpu.VMEM((2, K), i32), pltpu.VMEM((K, F), bf16),
            pltpu.VMEM((1, 1), i32), pltpu.VMEM((1, K), i32),
            pltpu.VMEM((SIDE, SIDE, F), bf16), pltpu.VMEM((SIDE, SIDE, F), bf16),
            *[pltpu.VMEM((K, PIX), bf16) for _ in range(8)],
            *[pltpu.VMEM((K, F), bf16) for _ in range(4)], pltpu.VMEM((9, K, F), bf16),
            pltpu.VMEM((3, ROWS, F), f32), pltpu.VMEM((3, 5, 3, ROWS, F), f32),
            *[pltpu.VMEM((K, F), f32) for _ in range(4)],
            *[pltpu.VMEM((2 * FIRST, K), f32) for _ in range(4)],
            pltpu.VMEM((ROWS, 9 * ROWS), f32), pltpu.VMEM((9, ROWS, 9 * ROWS), f32),
            pltpu.VMEM((2 * ROWS, F), f32), pltpu.VMEM((9, 2 * ROWS, F), f32),
            pltpu.VMEM((len(RING), ROWS, F), f32),
            pltpu.SemaphoreType.DMA((7,)),
            pltpu.SemaphoreType.DMA((messages,)), pltpu.SemaphoreType.DMA((messages,)),
        ],
        compiler_params=pltpu.CompilerParams(collective_id=0, has_side_effects=True),
    )(movie, footprints[0, 0], centres[0, 0].T, traces[0, 0], counts, order[0])
    return result[None, None]


def solution(mesh):
    in_specs = (
        P("ty", "tx", None),
        P("ty", "tx", None, None),
        P("ty", "tx", None, None),
        P("ty", "tx", None, None),
        P("ty", "tx"),
        P("ty", "tx", None),
    )
    out_specs = P("ty", "tx", None, None)
    return jax.shard_map(body, mesh=mesh, in_specs=in_specs, out_specs=out_specs, check_vma=False)
```

time: 50.6 us -> 39.9 us (0.79)
  Pallas kernels: 47 us -> 38.4 us
  local copies, waits for them, and re-layouts: 2.69 us -> 0.61 us
    pallas_call x1, Pallas kernels: 47 us -> 38.4 us  [body(): pl.pallas_call(kernel, name='hals', out_shape=pltpu.VMEM((K, F), f32), in...]
    unnamed x3 -> x1, local copies, waits for them, and re-layouts: 2 us -> 0.61 us
    squeeze x1 -> x0, local copies, waits for them, and re-layouts: 0.69 us -> none  [body(): centres[0, 0]]
where the time goes in v2:
time: 39.9 us; the launch traced here: 39.7 us
  Pallas kernels  38.4 us (96%)
  between operations  0.66 us (2%)
  local copies, waits for them, and re-layouts  0.61 us (2%)
    pallas_call x1, Pallas kernels, body(): pl.pallas_call(kernel, name='hals', out_shape=pltpu.VMEM((K, F), f32), in...  38.4 us

profile of v2, /device:TPU:7, one launch (start us, length us, event | category | flops | bytes accessed | tf_op | source)
XLA Modules:
  0.0 39.7 jit_solution(10686401597672428748)
XLA Ops:
  0.7 38.4 %hals.1 = f32[32,128]{1,0:T(8,128)S(1)} custom-call(bf16[32,32,128]{2,1,0:T(8,128)(2,1)} %movie.1, bf16[32,1024]{1,0:T(8,128)(2,1)} %bitcast.8, s32[2,32]{1,0:T(2,128)} %bitcast.10, bf16[32,128]{1,0:T(8,128)(2,1)} %bitcast.9, s32[1,1]{1,0:T(1,128)S(6)} %copy.9.counts_in, s32[1,32]{1,0:T(1,128)} %bitcast.11), custom_call_target="tpu_custom_call" | custom-call | tf_op jit(solution)/shard_map/hals/pallas_call | solution.py:439
  39.1 0.6 %copy.8 = f32[1,1,32,128]{3,2,1,0:T(8,128)} copy(f32[1,1,32,128]{3,2,1,0:T(8,128)S(1)} %bitcast.7) | data formatting | bytes 32768

commit v3 on v2

--- a/solution.py
+++ b/solution.py
@@ -12,12 +12,12 @@
 HALF = SIDE // 2
 ROWS = 8
 BLOCKS = 4
-FIRST = 24
 MESH = pl.DeviceIdType.MESH
 NEAR = [(u, v) for u in (-1, 0, 1) for v in (-1, 0, 1)]
 WIDE = [(u, v) for u in range(-2, 3) for v in range(-2, 3)]
 RING = [o for o in WIDE if o not in NEAR]
-BAND = [(u, v) for u in (-1, 0, 1) for v in range(-2, 3) if (u, v) != (0, 0)]
+BAND = [(u, v) for v in (-1, 1, -2, 2, 0) for u in (0, -1, 1) if (u, v) != (0, 0)]
+OUTWARD = [(u, v) for v in (-1, 1, -2, 2, 0) for u in (0, -1, 1, -2, 2) if (u, v) != (0, 0)]
 HERE = (0, 0)
 f32, bf16, i32 = jnp.float32, jnp.bfloat16, jnp.int32
 UP, DOWN, LEFT, RIGHT = (-1, 0), (1, 0), (0, -1), (0, 1)
@@ -81,7 +81,7 @@
 
     barrier = pltpu.get_barrier_semaphore()
     expected = jnp.int32(0)
-    for o in WIDE:
+    for o in NEAR:
         if o == HERE:
             continue
         present = there(o)
@@ -142,9 +142,10 @@
     clear(RIGHT, from_right, sum_from_right)
     for o in NEAR:
         if o != HERE:
-            clear(o, infos.at[slot(o)], margins.at[slot(o)], steps.at[slot(o)])
+            clear(o, infos.at[0, slot(o)], infos.at[1, slot(o)], margins.at[slot(o)])
+            clear(o, steps.at[slot(o)])
     for o in BAND:
-        clear(o, abouts.at[o[0] + 1, o[1] + 2])
+        clear(o, *[abouts.at[i, o[0] + 1, o[1] + 2] for i in range(2)])
     for o in RING:
         clear(o, far_steps.at[RING.index(o)])
 
@@ -179,10 +180,10 @@
     level_parts = jnp.where(
         wide_lane == 0, level_high, jnp.where(wide_lane == 1, level_mid, level_low)
     )
-    info[...] = jnp.concatenate(
-        [start_value[:ROWS], start_value[2 * ROWS:3 * ROWS],
-         level_parts[:ROWS], level_parts[2 * ROWS:3 * ROWS]], axis=0
-    ).astype(bf16)
+    for i, q in enumerate((0, 2)):
+        info[i] = jnp.concatenate(
+            [x[q * ROWS:(q + 1) * ROWS] for x in (start_value, level_parts)], axis=0
+        ).astype(bf16)
 
     group, across = wide_lane >> 5, wide_lane & 31
     turn, shift = (row_at + HALF) & 31, (col_at + HALF) & 31
@@ -212,11 +213,13 @@
 
     pl.semaphore_wait(barrier, expected)
 
-    early, late = pl.ds(0, FIRST), pl.ds(FIRST, K - FIRST)
-    side, side_late = [
-        [Remote(to_left.at[rows], from_right.at[rows], LEFT),
-         Remote(to_right.at[rows], from_left.at[rows], RIGHT)]
-        for rows in (early, late)
+    def chunk(q):
+        return pl.ds(q * ROWS, ROWS)
+
+    side = [
+        [Remote(to_left.at[chunk(q)], from_right.at[chunk(q)], LEFT),
+         Remote(to_right.at[chunk(q)], from_left.at[chunk(q)], RIGHT)]
+        for q in range(BLOCKS)
     ]
     vertical = [
         Remote(to_up, from_down, UP), Remote(to_down, from_up, DOWN),
@@ -224,8 +227,11 @@
         Remote(top_movie.at[pl.ds(0, HALF)], bottom_movie.at[pl.ds(0, HALF)], UP),
         Remote(bottom_movie.at[pl.ds(HALF, HALF)], top_movie.at[pl.ds(HALF, HALF)], DOWN),
     ]
-    known = [Remote(info, infos.at[slot(flip(o))], o) for o in NEAR if o != HERE]
-    for message in side + vertical + side_late + known:
+    known = [
+        [Remote(info.at[i], infos.at[i, slot(flip(o))], o) for o in NEAR if o != HERE]
+        for i in range(2)
+    ]
+    for message in side[0] + side[1] + vertical + side[2] + known[0]:
         message.start()
 
     own_tl, own_bl = positive(to_left[...]), positive(-to_left[...])
@@ -266,28 +272,44 @@
         r = nn(r_tl, rest_tr) + nn(r_bl, rest_br)
         return l[:, :F] + l[:, F:], r[:, :F] + r[:, F:]
 
-    for message in side:
-        message.arrived()
-    parts = halves(early)
-    l_sum, r_sum = side_sums(*parts)
-    about[0], about[1], about[2] = l_sum[:ROWS], total[:ROWS], r_sum[:ROWS]
-    sum_left[:FIRST, :], sum_right[:FIRST, :] = l_sum, r_sum
-    first_sums = []
-    for o in BAND:
-        low, high = max(0, o[1]), min(3, 3 + o[1])
-        first_sums.append(
-            Remote(
-                about.at[pl.ds(low, high - low)],
-                abouts.at[1 - o[0], 2 - o[1], pl.ds(low - o[1], high - low)], o,
-            ).start()
-        )
-    middle = pl.ds(ROWS, FIRST - ROWS)
-    returned = [
-        Remote(sum_left.at[middle], sum_from_right.at[middle], LEFT).start(),
-        Remote(sum_right.at[middle], sum_from_left.at[middle], RIGHT).start(),
-    ]
-
-    l_tr, l_br, r_tl, r_bl = parts
+    def side_parts(q):
+        for message in side[q]:
+            message.arrived()
+        parts = halves(slice(q * ROWS, (q + 1) * ROWS))
+        return parts, side_sums(*parts)
+
+    def to_band(i, q, l_sum, r_sum):
+        about[i, 0], about[i, 1], about[i, 2] = l_sum, total[q * ROWS:(q + 1) * ROWS], r_sum
+        messages = []
+        for o in BAND:
+            low, high = max(0, o[1]), min(3, 3 + o[1])
+            messages.append(
+                Remote(
+                    about.at[i, pl.ds(low, high - low)],
+                    abouts.at[i, 1 - o[0], 2 - o[1], pl.ds(low - o[1], high - low)], o,
+                ).start()
+            )
+        return messages
+
+    def give_back(i, l_sum, r_sum):
+        sum_left[i], sum_right[i] = l_sum, r_sum
+        return [
+            Remote(sum_left.at[i], sum_from_right.at[i], LEFT).start(),
+            Remote(sum_right.at[i], sum_from_left.at[i], RIGHT).start(),
+        ]
+
+    parts0, sums = side_parts(0)
+    band = [to_band(0, 0, *sums)]
+    parts1, sums = side_parts(1)
+    returned = give_back(0, *sums)
+    for message in side[3] + known[1]:
+        message.start()
+    parts2, sums = side_parts(2)
+    band.append(to_band(1, 2, *sums))
+
+    l_tr, l_br, r_tl, r_bl = (
+        jnp.concatenate(x, axis=0) for x in zip(parts0, parts1, parts2)
+    )
     gram_tl, gram_bl = nt(l_tr, stack_tl), nt(l_br, stack_bl)
     gram_tr, gram_br = nt(r_tl, stack_tr), nt(r_bl, stack_br)
     cross_up[...] = jnp.concatenate([gram_tl[:, K:], gram_tr[:, K:]], axis=0)
@@ -303,21 +325,12 @@
     own_own = own_top[:K] + own_bottom[:K]
     own_up, own_down = own_top[K:], own_bottom[K:]
 
-    for message in side_late:
-        message.arrived()
-    l_sum, r_sum = side_sums(*halves(late))
-    sum_left[FIRST:, :], sum_right[FIRST:, :] = l_sum, r_sum
-    returned_late = [
-        Remote(sum_left.at[late], sum_from_right.at[late], LEFT).start(),
-        Remote(sum_right.at[late], sum_from_left.at[late], RIGHT).start(),
-    ]
-
     for message in crossing:
         message.arrived()
     around = [
-        cross_from_up[:FIRST, :], own_up, cross_from_up[FIRST:, :],
+        cross_from_up[:3 * ROWS, :], own_up, cross_from_up[3 * ROWS:, :],
         own_left, own_own, own_right,
-        cross_from_down[:FIRST, :], own_down, cross_from_down[FIRST:, :],
+        cross_from_down[:3 * ROWS, :], own_down, cross_from_down[3 * ROWS:, :],
     ]
     columns = [
         jnp.concatenate([m[q * ROWS:(q + 1) * ROWS] for m in around], axis=0).T
@@ -333,61 +346,64 @@
     def rows(q):
         return slice(q * ROWS, (q + 1) * ROWS)
 
-    for message in known:
-        message.arrived()
-    facts = {}
-    for o in NEAR:
-        if o == HERE:
-            facts[o] = [start_value[rows(0)], start_value[rows(2)], divisor[rows(0)], divisor[rows(2)]]
-            continue
-        x = infos[slot(o)].astype(f32)
-        level = x[:, 0:1] + x[:, 1:2] + x[:, 2:3]
-        levels = (jnp.where(y == 0.0, 1.0, y) for y in (level[rows(2)], level[rows(3)]))
-        facts[o] = [x[rows(0)], x[rows(1)], *levels]
-
-    for message in first_sums:
-        message.arrived()
-    moved = []
-    for o in NEAR:
+    def facts(i, q):
+        for message in known[i]:
+            message.arrived()
+        found = {HERE: (start_value[rows(q)], divisor[rows(q)])}
+        for o in NEAR:
+            if o != HERE:
+                x = infos[i, slot(o)].astype(f32)
+                level = x[ROWS:, 0:1] + x[ROWS:, 1:2] + x[ROWS:, 2:3]
+                found[o] = (x[:ROWS], jnp.where(level == 0.0, 1.0, level))
+        return found
+
+    def band_sum(i, o):
         left_over = None
         for v in range(-2, 3):
             if abs(v - o[1]) > 1:
                 continue
             piece = (
-                about[o[1] + 1] if (o[0], v) == HERE
-                else abouts[o[0] + 1, v + 2, o[1] + 1]
+                about[i, o[1] + 1] if (o[0], v) == HERE
+                else abouts[i, o[0] + 1, v + 2, o[1] + 1]
             )
             left_over = piece if left_over is None else left_over + piece
-        previous = facts[o][0]
-        renewed = stepped(previous, left_over, facts[o][2])
+        return left_over
+
+    known_now = facts(0, 0)
+    for message in band[0]:
+        message.arrived()
+    moved = []
+    for o in NEAR:
+        previous, level = known_now[o]
+        renewed = stepped(previous, band_sum(0, o), level)
         if o == HERE:
             renewed = jnp.where(alive_col[rows(0)], renewed, 0.0)
             current = [renewed]
         moved.append(renewed - previous)
+    change = nn(columns[0][ROWS:], rows_of(jnp.concatenate(moved, axis=0)))
+
     for message in returned:
         message.arrived()
-    total = total[ROWS:FIRST] + sum_from_left[ROWS:FIRST, :] + sum_from_right[ROWS:FIRST, :]
-    change = nn(columns[0][ROWS:], rows_of(jnp.concatenate(moved, axis=0)))
-    total = total - change[:FIRST - ROWS]
-
+    left_over = total[rows(1)] + sum_from_left[0] + sum_from_right[0] - change[:ROWS]
     previous = start_value[rows(1)]
-    renewed = stepped(previous, total[:ROWS], divisor[rows(1)])
+    renewed = stepped(previous, left_over, divisor[rows(1)])
     renewed = jnp.where(alive_col[rows(1)], renewed, 0.0)
     current.append(renewed)
     own_step = renewed - previous
     step[:ROWS, :] = own_step
-    step[ROWS:, :] = total[ROWS:]
+    step[ROWS:, :] = change[ROWS:2 * ROWS]
     moves = [
         Remote(step, steps.at[slot(flip(o))], o).start() if o in NEAR
         else Remote(
             step.at[pl.ds(0, ROWS)], far_steps.at[RING.index(flip(o))], o
         ).start()
-        for o in WIDE if o != HERE
-    ]
-    for message in returned_late:
-        message.arrived()
-    last = both[FIRST:, :F] + both[FIRST:, F:] + sum_from_left[FIRST:, :]
-    last = last + sum_from_right[FIRST:, :] - change[FIRST - ROWS:]
+        for o in OUTWARD
+    ]
+    _, sums = side_parts(3)
+    returned_late = give_back(1, *sums)
+    known_now = facts(1, 2)
+    for message in band[1]:
+        message.arrived()
     for message in lent:
         message.arrived()
     weights = {
@@ -406,19 +422,24 @@
     for o in NEAR:
         nearby = rows_of(jnp.concatenate([taken[plus(o, p)] for p in NEAR], axis=0))
         if o == HERE:
-            left_over = total[ROWS:]
-            last = last - nn(columns[1][FIRST:], nearby)
+            left_over = band_sum(1, o) - change[ROWS:2 * ROWS]
+            last_change = change[2 * ROWS:] + nn(columns[1][3 * ROWS:], nearby)
         else:
-            left_over = steps[slot(o), ROWS:, :]
+            left_over = band_sum(1, o) - steps[slot(o), ROWS:, :]
         left_over = left_over - nn(weights[o], nearby)
-        previous = facts[o][1]
-        renewed = stepped(previous, left_over, facts[o][3])
+        previous, level = known_now[o]
+        renewed = stepped(previous, left_over, level)
         if o == HERE:
             renewed = jnp.where(alive_col[rows(2)], renewed, 0.0)
             current.append(renewed)
         moved.append(renewed - previous)
 
-    last = last - nn(columns[2][FIRST:], rows_of(jnp.concatenate(moved, axis=0)))
+    last_change = last_change + nn(
+        columns[2][3 * ROWS:], rows_of(jnp.concatenate(moved, axis=0))
+    )
+    for message in returned_late:
+        message.arrived()
+    last = total[rows(3)] + sum_from_left[1] + sum_from_right[1] - last_change
     renewed = stepped(start_value[rows(3)], last, divisor[rows(3)])
     current.append(jnp.where(alive_col[rows(3)], renewed, 0.0))
     result = jnp.concatenate(current, axis=0)
@@ -434,7 +455,7 @@
 
 
 def body(movie, footprints, centres, traces, counts, order):
-    messages = 4 + 6 + 8 + len(BAND) + 4 + 2 + 8 + 24
+    messages = 8 + 6 + 16 + 2 * len(BAND) + 4 + 2 + 8 + 24
     any_space = pl.BlockSpec(memory_space=pl.ANY)
     result = pl.pallas_call(
         kernel,
@@ -447,10 +468,11 @@
             pltpu.VMEM((1, 1), i32), pltpu.VMEM((1, K), i32),
             pltpu.VMEM((SIDE, SIDE, F), bf16), pltpu.VMEM((SIDE, SIDE, F), bf16),
             *[pltpu.VMEM((K, PIX), bf16) for _ in range(8)],
-            *[pltpu.VMEM((K, F), bf16) for _ in range(4)], pltpu.VMEM((9, K, F), bf16),
-            pltpu.VMEM((3, ROWS, F), f32), pltpu.VMEM((3, 5, 3, ROWS, F), f32),
-            *[pltpu.VMEM((K, F), f32) for _ in range(4)],
-            *[pltpu.VMEM((2 * FIRST, K), f32) for _ in range(4)],
+            *[pltpu.VMEM((K, F), bf16) for _ in range(3)],
+            pltpu.VMEM((2, 2 * ROWS, F), bf16), pltpu.VMEM((2, 9, 2 * ROWS, F), bf16),
+            pltpu.VMEM((2, 3, ROWS, F), f32), pltpu.VMEM((2, 3, 5, 3, ROWS, F), f32),
+            *[pltpu.VMEM((2, ROWS, F), f32) for _ in range(4)],
+            *[pltpu.VMEM((6 * ROWS, K), f32) for _ in range(4)],
             pltpu.VMEM((ROWS, 9 * ROWS), f32), pltpu.VMEM((9, ROWS, 9 * ROWS), f32),
             pltpu.VMEM((2 * ROWS, F), f32), pltpu.VMEM((9, 2 * ROWS, F), f32),
             pltpu.VMEM((len(RING), ROWS, F), f32),

time: 39.9 us -> 40.4 us (1.013)
  Pallas kernels: 38.4 us -> 38.9 us
    pallas_call x1, Pallas kernels: 38.4 us -> 38.9 us  [body(): pl.pallas_call(kernel, name='hals', out_shape=pltpu.VMEM((K, F), f32), in...]
where the time goes in v3:
time: 40.4 us; the launch traced here: 40.2 us
  Pallas kernels  38.9 us (96%)
  between operations  0.66 us (2%)
  local copies, waits for them, and re-layouts  0.61 us (2%)
    pallas_call x1, Pallas kernels, body(): pl.pallas_call(kernel, name='hals', out_shape=pltpu.VMEM((K, F), f32), in...  38.9 us

profile of v3, /device:TPU:7, one launch (start us, length us, event | category | flops | bytes accessed | tf_op | source)
XLA Modules:
  0.0 40.2 jit_solution(14720263164964399501)
XLA Ops:
  0.7 38.9 %hals.1 = f32[32,128]{1,0:T(8,128)S(1)} custom-call(bf16[32,32,128]{2,1,0:T(8,128)(2,1)} %movie.1, bf16[32,1024]{1,0:T(8,128)(2,1)} %bitcast.8, s32[2,32]{1,0:T(2,128)} %bitcast.10, bf16[32,128]{1,0:T(8,128)(2,1)} %bitcast.9, s32[1,1]{1,0:T(1,128)S(6)} %copy.9.counts_in, s32[1,32]{1,0:T(1,128)} %bitcast.11), custom_call_target="tpu_custom_call" | custom-call | tf_op jit(solution)/shard_map/hals/pallas_call | solution.py:460
  39.6 0.6 %copy.8 = f32[1,1,32,128]{3,2,1,0:T(8,128)} copy(f32[1,1,32,128]{3,2,1,0:T(8,128)S(1)} %bitcast.7) | data formatting | bytes 32768

commit v4 on v3

--- a/solution.py
+++ b/solution.py
@@ -66,10 +66,10 @@
     foot, centres, traces, counts, order,
     top_movie, bottom_movie, to_left, to_right, to_up, to_down,
     from_right, from_left, from_down, from_up,
-    start, start_up, start_down, info, infos,
+    start, start_up, start_down, infos,
     about, abouts, sum_left, sum_right, sum_from_right, sum_from_left,
     cross_up, cross_down, cross_from_down, cross_from_up,
-    margin, margins, step, steps, far_steps,
+    margins, step, steps, far_steps,
     local_sem, send_sem, recv_sem,
 ):
     a, b = lax.axis_index("ty"), lax.axis_index("tx")
@@ -142,10 +142,13 @@
     clear(RIGHT, from_right, sum_from_right)
     for o in NEAR:
         if o != HERE:
-            clear(o, infos.at[0, slot(o)], infos.at[1, slot(o)], margins.at[slot(o)])
             clear(o, steps.at[slot(o)])
+    for o in (UP, DOWN):
+        clear(o, infos.at[o[0] + 1], margins.at[o[0] + 1])
+    for o in (LEFT, RIGHT):
+        clear(o, infos.at[1, o[1] + 1], margins.at[1, o[1] + 1])
     for o in BAND:
-        clear(o, *[abouts.at[i, o[0] + 1, o[1] + 2] for i in range(2)])
+        clear(o, abouts.at[o[0] + 1, o[1] + 2])
     for o in RING:
         clear(o, far_steps.at[RING.index(o)])
 
@@ -181,7 +184,7 @@
         wide_lane == 0, level_high, jnp.where(wide_lane == 1, level_mid, level_low)
     )
     for i, q in enumerate((0, 2)):
-        info[i] = jnp.concatenate(
+        infos[1, 1, i] = jnp.concatenate(
             [x[q * ROWS:(q + 1) * ROWS] for x in (start_value, level_parts)], axis=0
         ).astype(bf16)
 
@@ -227,12 +230,17 @@
         Remote(top_movie.at[pl.ds(0, HALF)], bottom_movie.at[pl.ds(0, HALF)], UP),
         Remote(bottom_movie.at[pl.ds(HALF, HALF)], top_movie.at[pl.ds(HALF, HALF)], DOWN),
     ]
-    known = [
-        [Remote(info.at[i], infos.at[i, slot(flip(o))], o) for o in NEAR if o != HERE]
-        for i in range(2)
-    ]
-    for message in side[0] + side[1] + vertical + side[2] + known[0]:
+    def along(ref):
+        return [Remote(ref.at[1, 1], ref.at[1, 1 - o[1]], o).start() for o in (LEFT, RIGHT)]
+
+    def across(ref, messages):
+        for message in messages:
+            message.arrived()
+        return [Remote(ref.at[1], ref.at[1 - o[0]], o).start() for o in (UP, DOWN)]
+
+    for message in side[0] + vertical + side[1] + side[2]:
         message.start()
+    known = along(infos)
 
     own_tl, own_bl = positive(to_left[...]), positive(-to_left[...])
     own_tr, own_br = positive(to_right[...]), positive(-to_right[...])
@@ -278,15 +286,15 @@
         parts = halves(slice(q * ROWS, (q + 1) * ROWS))
         return parts, side_sums(*parts)
 
-    def to_band(i, q, l_sum, r_sum):
-        about[i, 0], about[i, 1], about[i, 2] = l_sum, total[q * ROWS:(q + 1) * ROWS], r_sum
+    def to_band(l_sum, r_sum):
+        about[0], about[1], about[2] = l_sum, total[:ROWS], r_sum
         messages = []
         for o in BAND:
             low, high = max(0, o[1]), min(3, 3 + o[1])
             messages.append(
                 Remote(
-                    about.at[i, pl.ds(low, high - low)],
-                    abouts.at[i, 1 - o[0], 2 - o[1], pl.ds(low - o[1], high - low)], o,
+                    about.at[pl.ds(low, high - low)],
+                    abouts.at[1 - o[0], 2 - o[1], pl.ds(low - o[1], high - low)], o,
                 ).start()
             )
         return messages
@@ -298,47 +306,50 @@
             Remote(sum_right.at[i], sum_from_left.at[i], RIGHT).start(),
         ]
 
-    parts0, sums = side_parts(0)
-    band = [to_band(0, 0, *sums)]
-    parts1, sums = side_parts(1)
-    returned = give_back(0, *sums)
-    for message in side[3] + known[1]:
+    def meet(q, l_tr, l_br, r_tl, r_bl):
+        gram_tl, gram_bl = nt(l_tr, stack_tl), nt(l_br, stack_bl)
+        gram_tr, gram_br = nt(r_tl, stack_tr), nt(r_bl, stack_br)
+        cross_up[q] = jnp.concatenate([gram_tl[:, K:], gram_tr[:, K:]], axis=0)
+        cross_down[q] = jnp.concatenate([gram_bl[:, K:], gram_br[:, K:]], axis=0)
+        crossing = [
+            Remote(cross_up.at[q], cross_from_down.at[q], UP).start(),
+            Remote(cross_down.at[q], cross_from_up.at[q], DOWN).start(),
+        ]
+        return crossing, gram_tl[:, :K] + gram_bl[:, :K], gram_tr[:, :K] + gram_br[:, :K]
+
+    met, returned = [], []
+    for q in range(BLOCKS - 1):
+        parts, sums = side_parts(q)
+        if q == 0:
+            band = to_band(*sums)
+        else:
+            returned += give_back(q - 1, *sums)
+        met.append(meet(q, *parts))
+    for message in side[3]:
         message.start()
-    parts2, sums = side_parts(2)
-    band.append(to_band(1, 2, *sums))
-
-    l_tr, l_br, r_tl, r_bl = (
-        jnp.concatenate(x, axis=0) for x in zip(parts0, parts1, parts2)
-    )
-    gram_tl, gram_bl = nt(l_tr, stack_tl), nt(l_br, stack_bl)
-    gram_tr, gram_br = nt(r_tl, stack_tr), nt(r_bl, stack_br)
-    cross_up[...] = jnp.concatenate([gram_tl[:, K:], gram_tr[:, K:]], axis=0)
-    cross_down[...] = jnp.concatenate([gram_bl[:, K:], gram_br[:, K:]], axis=0)
-    crossing = [
-        Remote(cross_up, cross_from_down, UP).start(),
-        Remote(cross_down, cross_from_up, DOWN).start(),
-    ]
-    own_left = gram_tl[:, :K] + gram_bl[:, :K]
-    own_right = gram_tr[:, :K] + gram_br[:, :K]
     own_top = nt(stack_tl, own_tl) + nt(stack_tr, own_tr)
     own_bottom = nt(stack_bl, own_bl) + nt(stack_br, own_br)
     own_own = own_top[:K] + own_bottom[:K]
     own_up, own_down = own_top[K:], own_bottom[K:]
 
-    for message in crossing:
-        message.arrived()
-    around = [
-        cross_from_up[:3 * ROWS, :], own_up, cross_from_up[3 * ROWS:, :],
-        own_left, own_own, own_right,
-        cross_from_down[:3 * ROWS, :], own_down, cross_from_down[3 * ROWS:, :],
-    ]
-    columns = [
-        jnp.concatenate([m[q * ROWS:(q + 1) * ROWS] for m in around], axis=0).T
-        for q in range(BLOCKS - 1)
-    ]
-    margin[...] = columns[1][2 * ROWS:3 * ROWS]
-    lent = [Remote(margin, margins.at[slot(flip(o))], o).start() for o in NEAR if o != HERE]
-    columns = [lanes_of(x) for x in columns]
+    def column(q):
+        crossing, own_left, own_right = met[q]
+        for message in crossing:
+            message.arrived()
+        mine = slice(q * ROWS, (q + 1) * ROWS)
+        above, below = cross_from_up[q], cross_from_down[q]
+        return jnp.concatenate(
+            [above[:ROWS], own_up[mine], above[ROWS:], own_left, own_own[mine], own_right,
+             below[:ROWS], own_down[mine], below[ROWS:]], axis=0
+        ).T
+
+    columns = [None] * (BLOCKS - 1)
+    known = across(infos, known)
+    columns[1] = column(1)
+    margins[1, 1] = columns[1][2 * ROWS:3 * ROWS]
+    lent = along(margins)
+    columns[1] = lanes_of(columns[1])
+    columns[0] = lanes_of(column(0))
 
     def stepped(previous, left_over, level):
         return jnp.maximum(previous + left_over / level, 0.0)
@@ -347,35 +358,35 @@
         return slice(q * ROWS, (q + 1) * ROWS)
 
     def facts(i, q):
-        for message in known[i]:
-            message.arrived()
         found = {HERE: (start_value[rows(q)], divisor[rows(q)])}
         for o in NEAR:
             if o != HERE:
-                x = infos[i, slot(o)].astype(f32)
+                x = infos[o[0] + 1, o[1] + 1, i].astype(f32)
                 level = x[ROWS:, 0:1] + x[ROWS:, 1:2] + x[ROWS:, 2:3]
                 found[o] = (x[:ROWS], jnp.where(level == 0.0, 1.0, level))
         return found
 
-    def band_sum(i, o):
+    def band_sum(o):
         left_over = None
         for v in range(-2, 3):
             if abs(v - o[1]) > 1:
                 continue
             piece = (
-                about[i, o[1] + 1] if (o[0], v) == HERE
-                else abouts[i, o[0] + 1, v + 2, o[1] + 1]
+                about[o[1] + 1] if (o[0], v) == HERE
+                else abouts[o[0] + 1, v + 2, o[1] + 1]
             )
             left_over = piece if left_over is None else left_over + piece
         return left_over
 
+    for message in known:
+        message.arrived()
     known_now = facts(0, 0)
-    for message in band[0]:
+    for message in band:
         message.arrived()
     moved = []
     for o in NEAR:
         previous, level = known_now[o]
-        renewed = stepped(previous, band_sum(0, o), level)
+        renewed = stepped(previous, band_sum(o), level)
         if o == HERE:
             renewed = jnp.where(alive_col[rows(0)], renewed, 0.0)
             current = [renewed]
@@ -391,7 +402,8 @@
     current.append(renewed)
     own_step = renewed - previous
     step[:ROWS, :] = own_step
-    step[ROWS:, :] = change[ROWS:2 * ROWS]
+    own_sum = total[rows(2)] + sum_from_left[1] + sum_from_right[1] - change[ROWS:2 * ROWS]
+    step[ROWS:, :] = own_sum
     moves = [
         Remote(step, steps.at[slot(flip(o))], o).start() if o in NEAR
         else Remote(
@@ -399,15 +411,15 @@
         ).start()
         for o in OUTWARD
     ]
+    lent = across(margins, lent)
     _, sums = side_parts(3)
-    returned_late = give_back(1, *sums)
+    returned_late = give_back(2, *sums)
+    columns[2] = lanes_of(column(2))
     known_now = facts(1, 2)
-    for message in band[1]:
-        message.arrived()
     for message in lent:
         message.arrived()
     weights = {
-        o: lanes_of(margin[...] if o == HERE else margins[slot(o)]) for o in NEAR
+        o: lanes_of(margins[o[0] + 1, o[1] + 1]) for o in NEAR
     }
 
     for message in moves:
@@ -422,10 +434,10 @@
     for o in NEAR:
         nearby = rows_of(jnp.concatenate([taken[plus(o, p)] for p in NEAR], axis=0))
         if o == HERE:
-            left_over = band_sum(1, o) - change[ROWS:2 * ROWS]
+            left_over = own_sum
             last_change = change[2 * ROWS:] + nn(columns[1][3 * ROWS:], nearby)
         else:
-            left_over = band_sum(1, o) - steps[slot(o), ROWS:, :]
+            left_over = steps[slot(o), ROWS:, :]
         left_over = left_over - nn(weights[o], nearby)
         previous, level = known_now[o]
         renewed = stepped(previous, left_over, level)
@@ -439,7 +451,7 @@
     )
     for message in returned_late:
         message.arrived()
-    last = total[rows(3)] + sum_from_left[1] + sum_from_right[1] - last_change
+    last = total[rows(3)] + sum_from_left[2] + sum_from_right[2] - last_change
     renewed = stepped(start_value[rows(3)], last, divisor[rows(3)])
     current.append(jnp.where(alive_col[rows(3)], renewed, 0.0))
     result = jnp.concatenate(current, axis=0)
@@ -455,7 +467,7 @@
 
 
 def body(movie, footprints, centres, traces, counts, order):
-    messages = 8 + 6 + 16 + 2 * len(BAND) + 4 + 2 + 8 + 24
+    messages = 8 + 6 + 4 + len(BAND) + 6 + 6 + 4 + 24
     any_space = pl.BlockSpec(memory_space=pl.ANY)
     result = pl.pallas_call(
         kernel,
@@ -469,11 +481,11 @@
             pltpu.VMEM((SIDE, SIDE, F), bf16), pltpu.VMEM((SIDE, SIDE, F), bf16),
             *[pltpu.VMEM((K, PIX), bf16) for _ in range(8)],
             *[pltpu.VMEM((K, F), bf16) for _ in range(3)],
-            pltpu.VMEM((2, 2 * ROWS, F), bf16), pltpu.VMEM((2, 9, 2 * ROWS, F), bf16),
-            pltpu.VMEM((2, 3, ROWS, F), f32), pltpu.VMEM((2, 3, 5, 3, ROWS, F), f32),
-            *[pltpu.VMEM((2, ROWS, F), f32) for _ in range(4)],
-            *[pltpu.VMEM((6 * ROWS, K), f32) for _ in range(4)],
-            pltpu.VMEM((ROWS, 9 * ROWS), f32), pltpu.VMEM((9, ROWS, 9 * ROWS), f32),
+            pltpu.VMEM((3, 3, 2, 2 * ROWS, F), bf16),
+            pltpu.VMEM((3, ROWS, F), f32), pltpu.VMEM((3, 5, 3, ROWS, F), f32),
+            *[pltpu.VMEM((3, ROWS, F), f32) for _ in range(4)],
+            *[pltpu.VMEM((3, 2 * ROWS, K), f32) for _ in range(4)],
+            pltpu.VMEM((3, 3, ROWS, 9 * ROWS), f32),
             pltpu.VMEM((2 * ROWS, F), f32), pltpu.VMEM((9, 2 * ROWS, F), f32),
             pltpu.VMEM((len(RING), ROWS, F), f32),
             pltpu.SemaphoreType.DMA((7,)),

time: 40.4 us -> 38.8 us (0.960)
  Pallas kernels: 38.9 us -> 37.5 us
    pallas_call x1, Pallas kernels: 38.9 us -> 37.5 us  [body(): pl.pallas_call(kernel, name='hals', out_shape=pltpu.VMEM((K, F), f32), in...]
where the time goes in v4:
time: 38.8 us; the launch traced here: 38.7 us
  Pallas kernels  37.5 us (97%)
  between operations  0.66 us (2%)
  local copies, waits for them, and re-layouts  0.61 us (2%)
    pallas_call x1, Pallas kernels, body(): pl.pallas_call(kernel, name='hals', out_shape=pltpu.VMEM((K, F), f32), in...  37.5 us

profile of v4, /device:TPU:7, one launch (start us, length us, event | category | flops | bytes accessed | tf_op | source)
XLA Modules:
  0.0 38.7 jit_solution(8777254009813875507)
XLA Ops:
  0.7 37.5 %hals.1 = f32[32,128]{1,0:T(8,128)S(1)} custom-call(bf16[32,32,128]{2,1,0:T(8,128)(2,1)} %movie.1, bf16[32,1024]{1,0:T(8,128)(2,1)} %bitcast.8, s32[2,32]{1,0:T(2,128)} %bitcast.10, bf16[32,128]{1,0:T(8,128)(2,1)} %bitcast.9, s32[1,1]{1,0:T(1,128)S(6)} %copy.9.counts_in, s32[1,32]{1,0:T(1,128)} %bitcast.11), custom_call_target="tpu_custom_call" | custom-call | tf_op jit(solution)/shard_map/hals/pallas_call | solution.py:472
  38.1 0.6 %copy.8 = f32[1,1,32,128]{3,2,1,0:T(8,128)} copy(f32[1,1,32,128]{3,2,1,0:T(8,128)S(1)} %bitcast.7) | data formatting | bytes 32768

commit v5 on v4

--- a/solution.py
+++ b/solution.py
@@ -69,7 +69,7 @@
     start, start_up, start_down, infos,
     about, abouts, sum_left, sum_right, sum_from_right, sum_from_left,
     cross_up, cross_down, cross_from_down, cross_from_up,
-    margins, step, steps, far_steps,
+    margins, step, steps, far_steps, left_sum, left_sums, recon,
     local_sem, send_sem, recv_sem,
 ):
     a, b = lax.axis_index("ty"), lax.axis_index("tx")
@@ -142,11 +142,12 @@
     clear(RIGHT, from_right, sum_from_right)
     for o in NEAR:
         if o != HERE:
-            clear(o, steps.at[slot(o)])
+            clear(o, steps.at[slot(o)], left_sums.at[slot(o)])
     for o in (UP, DOWN):
-        clear(o, infos.at[o[0] + 1], margins.at[o[0] + 1])
+        clear(o, infos.at[0, o[0] + 1], infos.at[1, o[0] + 1], margins.at[o[0] + 1])
     for o in (LEFT, RIGHT):
-        clear(o, infos.at[1, o[1] + 1], margins.at[1, o[1] + 1])
+        clear(o, infos.at[0, 1, o[1] + 1], infos.at[1, 1, o[1] + 1])
+        clear(o, margins.at[1, o[1] + 1])
     for o in BAND:
         clear(o, abouts.at[o[0] + 1, o[1] + 2])
     for o in RING:
@@ -184,7 +185,7 @@
         wide_lane == 0, level_high, jnp.where(wide_lane == 1, level_mid, level_low)
     )
     for i, q in enumerate((0, 2)):
-        infos[1, 1, i] = jnp.concatenate(
+        infos[i, 1, 1] = jnp.concatenate(
             [x[q * ROWS:(q + 1) * ROWS] for x in (start_value, level_parts)], axis=0
         ).astype(bf16)
 
@@ -240,36 +241,36 @@
 
     for message in side[0] + vertical + side[1] + side[2]:
         message.start()
-    known = along(infos)
+    known = along(infos.at[0])
 
     own_tl, own_bl = positive(to_left[...]), positive(-to_left[...])
     own_tr, own_br = positive(to_right[...]), positive(-to_right[...])
-    for message in vertical:
+    for i, quarter in enumerate((own_tl, own_tr, own_bl, own_br)):
+        recon[i] = tn(quarter, start[...])
+    for message in vertical[:4]:
         message.arrived()
     up_bl, up_br = positive(from_up[...]), positive(-from_up[...])
     down_tl, down_tr = positive(from_down[...]), positive(-from_down[...])
-    column_top = jnp.concatenate([start[...], start_up[...]], axis=0)
-    column_bottom = jnp.concatenate([start[...], start_down[...]], axis=0)
-    stack_tl = jnp.concatenate([own_tl, up_bl], axis=0)
-    stack_tr = jnp.concatenate([own_tr, up_br], axis=0)
-    stack_bl = jnp.concatenate([own_bl, down_tl], axis=0)
-    stack_br = jnp.concatenate([own_br, down_tr], axis=0)
+    for i, (quarter, trace) in enumerate(
+        ((up_bl, start_up), (up_br, start_up), (down_tl, start_down), (down_tr, start_down))
+    ):
+        recon[i] += tn(quarter, trace[...])
+    for message in vertical[4:]:
+        message.arrived()
 
     near_rows = (lax.broadcasted_iota(i32, (PIX, F), 0) & 31) < HALF
 
-    def residual(pixels, near, stack, column):
+    def residual(pixels, near, i):
         seen = pixels[...].reshape(PIX, F).astype(f32)
         seen = jnp.where(near_rows, seen, 0.0) if near else jnp.where(near_rows, 0.0, seen)
-        rest = seen - tn(stack, column)
+        rest = seen - recon[i]
         high = rounded(rest)
         return jnp.concatenate([high, rest - high], axis=1).astype(bf16)
 
-    rest_tl = residual(top_movie, True, stack_tl, column_top)
-    rest_tr = residual(top_movie, False, stack_tr, column_top)
-    rest_bl = residual(bottom_movie, True, stack_bl, column_bottom)
-    rest_br = residual(bottom_movie, False, stack_br, column_bottom)
-    both = nn(own_tl, rest_tl) + nn(own_tr, rest_tr) + nn(own_bl, rest_bl) + nn(own_br, rest_br)
-    total = both[:, :F] + both[:, F:]
+    rest_tl = residual(top_movie, True, 0)
+    rest_tr = residual(top_movie, False, 1)
+    rest_bl = residual(bottom_movie, True, 2)
+    rest_br = residual(bottom_movie, False, 3)
 
     def halves(rows):
         l, r = from_left[rows, :], from_right[rows, :]
@@ -283,11 +284,20 @@
     def side_parts(q):
         for message in side[q]:
             message.arrived()
-        parts = halves(slice(q * ROWS, (q + 1) * ROWS))
-        return parts, side_sums(*parts)
-
-    def to_band(l_sum, r_sum):
-        about[0], about[1], about[2] = l_sum, total[:ROWS], r_sum
+        return halves(slice(q * ROWS, (q + 1) * ROWS))
+
+    def to_band(l_tr, l_br, r_tl, r_bl):
+        tl, bl, tr, br = (
+            nn(jnp.concatenate([own[:ROWS], x], axis=0), rest)
+            for own, x, rest in (
+                (own_tl, l_tr, rest_tl), (own_bl, l_br, rest_bl),
+                (own_tr, r_tl, rest_tr), (own_br, r_bl, rest_br),
+            )
+        )
+        for i, x in enumerate(
+            (tl[ROWS:] + bl[ROWS:], (tl + tr + bl + br)[:ROWS], tr[ROWS:] + br[ROWS:])
+        ):
+            about[i] = x[:, :F] + x[:, F:]
         messages = []
         for o in BAND:
             low, high = max(0, o[1]), min(3, 3 + o[1])
@@ -319,14 +329,21 @@
 
     met, returned = [], []
     for q in range(BLOCKS - 1):
-        parts, sums = side_parts(q)
+        parts = side_parts(q)
         if q == 0:
-            band = to_band(*sums)
+            band = to_band(*parts)
+            stack_tl = jnp.concatenate([own_tl, up_bl], axis=0)
+            stack_tr = jnp.concatenate([own_tr, up_br], axis=0)
+            stack_bl = jnp.concatenate([own_bl, down_tl], axis=0)
+            stack_br = jnp.concatenate([own_br, down_tr], axis=0)
         else:
-            returned += give_back(q - 1, *sums)
+            returned.append(give_back(q - 1, *side_sums(*parts)))
         met.append(meet(q, *parts))
     for message in side[3]:
         message.start()
+    known_late = along(infos.at[1])
+    both = nn(own_tl, rest_tl) + nn(own_tr, rest_tr) + nn(own_bl, rest_bl) + nn(own_br, rest_br)
+    total = both[:, :F] + both[:, F:]
     own_top = nt(stack_tl, own_tl) + nt(stack_tr, own_tr)
     own_bottom = nt(stack_bl, own_bl) + nt(stack_br, own_br)
     own_own = own_top[:K] + own_bottom[:K]
@@ -344,7 +361,7 @@
         ).T
 
     columns = [None] * (BLOCKS - 1)
-    known = across(infos, known)
+    known = across(infos.at[0], known)
     columns[1] = column(1)
     margins[1, 1] = columns[1][2 * ROWS:3 * ROWS]
     lent = along(margins)
@@ -361,7 +378,7 @@
         found = {HERE: (start_value[rows(q)], divisor[rows(q)])}
         for o in NEAR:
             if o != HERE:
-                x = infos[o[0] + 1, o[1] + 1, i].astype(f32)
+                x = infos[i, o[0] + 1, o[1] + 1].astype(f32)
                 level = x[ROWS:, 0:1] + x[ROWS:, 1:2] + x[ROWS:, 2:3]
                 found[o] = (x[:ROWS], jnp.where(level == 0.0, 1.0, level))
         return found
@@ -393,7 +410,7 @@
         moved.append(renewed - previous)
     change = nn(columns[0][ROWS:], rows_of(jnp.concatenate(moved, axis=0)))
 
-    for message in returned:
+    for message in returned[0]:
         message.arrived()
     left_over = total[rows(1)] + sum_from_left[0] + sum_from_right[0] - change[:ROWS]
     previous = start_value[rows(1)]
@@ -401,20 +418,27 @@
     renewed = jnp.where(alive_col[rows(1)], renewed, 0.0)
     current.append(renewed)
     own_step = renewed - previous
-    step[:ROWS, :] = own_step
-    own_sum = total[rows(2)] + sum_from_left[1] + sum_from_right[1] - change[ROWS:2 * ROWS]
-    step[ROWS:, :] = own_sum
+    step[...] = own_step
     moves = [
-        Remote(step, steps.at[slot(flip(o))], o).start() if o in NEAR
-        else Remote(
-            step.at[pl.ds(0, ROWS)], far_steps.at[RING.index(flip(o))], o
+        Remote(
+            step,
+            steps.at[slot(flip(o))] if o in NEAR else far_steps.at[RING.index(flip(o))], o,
         ).start()
         for o in OUTWARD
     ]
+    for message in returned[1]:
+        message.arrived()
+    own_sum = total[rows(2)] + sum_from_left[1] + sum_from_right[1] - change[ROWS:2 * ROWS]
+    left_sum[...] = own_sum
+    moves += [
+        Remote(left_sum, left_sums.at[slot(flip(o))], o).start() for o in OUTWARD if o in NEAR
+    ]
+    returned_late = give_back(2, *side_sums(*side_parts(3)))
+    known_late = across(infos.at[1], known_late)
     lent = across(margins, lent)
-    _, sums = side_parts(3)
-    returned_late = give_back(2, *sums)
     columns[2] = lanes_of(column(2))
+    for message in known_late:
+        message.arrived()
     known_now = facts(1, 2)
     for message in lent:
         message.arrived()
@@ -422,11 +446,15 @@
         o: lanes_of(margins[o[0] + 1, o[1] + 1]) for o in NEAR
     }
 
+    sent_last = moves + returned_late
+    for message in sent:
+        if message not in sent_last:
+            message.left()
     for message in moves:
         message.arrived()
     taken = {
         o: own_step if o == HERE
-        else steps[slot(o), :ROWS, :] if o in NEAR
+        else steps[slot(o)] if o in NEAR
         else far_steps[RING.index(o)]
         for o in WIDE
     }
@@ -437,7 +465,7 @@
             left_over = own_sum
             last_change = change[2 * ROWS:] + nn(columns[1][3 * ROWS:], nearby)
         else:
-            left_over = steps[slot(o), ROWS:, :]
+            left_over = left_sums[slot(o)]
         left_over = left_over - nn(weights[o], nearby)
         previous, level = known_now[o]
         renewed = stepped(previous, left_over, level)
@@ -462,12 +490,12 @@
         jnp.concatenate([back, back, back], axis=1).astype(bf16),
         jnp.concatenate([high, mid, result - high - mid], axis=0).astype(bf16),
     )
-    for message in sent:
+    for message in sent_last:
         message.left()
 
 
 def body(movie, footprints, centres, traces, counts, order):
-    messages = 8 + 6 + 4 + len(BAND) + 6 + 6 + 4 + 24
+    messages = 8 + 6 + 8 + len(BAND) + 6 + 6 + 4 + 32
     any_space = pl.BlockSpec(memory_space=pl.ANY)
     result = pl.pallas_call(
         kernel,
@@ -481,13 +509,15 @@
             pltpu.VMEM((SIDE, SIDE, F), bf16), pltpu.VMEM((SIDE, SIDE, F), bf16),
             *[pltpu.VMEM((K, PIX), bf16) for _ in range(8)],
             *[pltpu.VMEM((K, F), bf16) for _ in range(3)],
-            pltpu.VMEM((3, 3, 2, 2 * ROWS, F), bf16),
+            pltpu.VMEM((2, 3, 3, 2 * ROWS, F), bf16),
             pltpu.VMEM((3, ROWS, F), f32), pltpu.VMEM((3, 5, 3, ROWS, F), f32),
             *[pltpu.VMEM((3, ROWS, F), f32) for _ in range(4)],
             *[pltpu.VMEM((3, 2 * ROWS, K), f32) for _ in range(4)],
             pltpu.VMEM((3, 3, ROWS, 9 * ROWS), f32),
-            pltpu.VMEM((2 * ROWS, F), f32), pltpu.VMEM((9, 2 * ROWS, F), f32),
+            pltpu.VMEM((ROWS, F), f32), pltpu.VMEM((9, ROWS, F), f32),
             pltpu.VMEM((len(RING), ROWS, F), f32),
+            pltpu.VMEM((ROWS, F), f32), pltpu.VMEM((9, ROWS, F), f32),
+            pltpu.VMEM((4, PIX, F), f32),
             pltpu.SemaphoreType.DMA((7,)),
             pltpu.SemaphoreType.DMA((messages,)), pltpu.SemaphoreType.DMA((messages,)),
         ],

time: 38.8 us -> 37.6 us (0.969)
  Pallas kernels: 37.5 us -> 36.3 us
    pallas_call x1, Pallas kernels: 37.5 us -> 36.3 us  [body(): pl.pallas_call(kernel, name='hals', out_shape=pltpu.VMEM((K, F), f32), in...]
where the time goes in v5:
time: 37.6 us; the launch traced here: 37.5 us
  Pallas kernels  36.3 us (97%)
  between operations  0.66 us (2%)
  local copies, waits for them, and re-layouts  0.61 us (2%)
    pallas_call x1, Pallas kernels, body(): pl.pallas_call(kernel, name='hals', out_shape=pltpu.VMEM((K, F), f32), in...  36.3 us

profile of v5, /device:TPU:7, one launch (start us, length us, event | category | flops | bytes accessed | tf_op | source)
XLA Modules:
  0.0 37.5 jit_solution(12184591657571634265)
XLA Ops:
  0.7 36.3 %hals.1 = f32[32,128]{1,0:T(8,128)S(1)} custom-call(bf16[32,32,128]{2,1,0:T(8,128)(2,1)} %movie.1, bf16[32,1024]{1,0:T(8,128)(2,1)} %bitcast.8, s32[2,32]{1,0:T(2,128)} %bitcast.10, bf16[32,128]{1,0:T(8,128)(2,1)} %bitcast.9, s32[1,1]{1,0:T(1,128)S(6)} %copy.9.counts_in, s32[1,32]{1,0:T(1,128)} %bitcast.11), custom_call_target="tpu_custom_call" | custom-call | tf_op jit(solution)/shard_map/hals/pallas_call | solution.py:500
  36.9 0.6 %copy.8 = f32[1,1,32,128]{3,2,1,0:T(8,128)} copy(f32[1,1,32,128]{3,2,1,0:T(8,128)S(1)} %bitcast.7) | data formatting | bytes 32768

commit v6 on v5

--- a/solution.py
+++ b/solution.py
@@ -15,9 +15,7 @@
 MESH = pl.DeviceIdType.MESH
 NEAR = [(u, v) for u in (-1, 0, 1) for v in (-1, 0, 1)]
 WIDE = [(u, v) for u in range(-2, 3) for v in range(-2, 3)]
-RING = [o for o in WIDE if o not in NEAR]
-BAND = [(u, v) for v in (-1, 1, -2, 2, 0) for u in (0, -1, 1) if (u, v) != (0, 0)]
-OUTWARD = [(u, v) for v in (-1, 1, -2, 2, 0) for u in (0, -1, 1, -2, 2) if (u, v) != (0, 0)]
+BAND = [(u, v) for u in (-1, 0, 1) for v in range(-2, 3) if (u, v) != (0, 0)]
 HERE = (0, 0)
 f32, bf16, i32 = jnp.float32, jnp.bfloat16, jnp.int32
 UP, DOWN, LEFT, RIGHT = (-1, 0), (1, 0), (0, -1), (0, 1)
@@ -69,7 +67,7 @@
     start, start_up, start_down, infos,
     about, abouts, sum_left, sum_right, sum_from_right, sum_from_left,
     cross_up, cross_down, cross_from_down, cross_from_up,
-    margins, step, steps, far_steps, left_sum, left_sums, recon,
+    margins, step, steps, left_sum, left_sums, recon,
     local_sem, send_sem, recv_sem,
 ):
     a, b = lax.axis_index("ty"), lax.axis_index("tx")
@@ -127,14 +125,54 @@
         def left(self):
             pl.when(there(self.o))(self.copy.wait_send)
 
+    class Fan:
+        def __init__(self, source, place, reach, v):
+            self.source, self.place, self.reach, self.v = source, place, reach, v
+            self.index = len(sent)
+            sent.append(self)
+
+        def copy(self, source, target, u):
+            return pltpu.make_async_remote_copy(
+                src_ref=source, dst_ref=target,
+                send_sem=send_sem.at[self.index], recv_sem=recv_sem.at[self.index],
+                device_id=(a + u, b + self.v), device_id_type=MESH,
+            )
+
+        def start(self):
+            for u in sorted(range(-self.reach, self.reach + 1), key=abs):
+                copy = self.copy(self.source, self.place(self.reach - u), u)
+                pl.when(there((u, self.v)))(copy.start)
+            return self
+
+        def wait(self, col, name):
+            reach = self.reach
+            rows = jnp.minimum(a, reach) + jnp.minimum(n_ty - 1 - a, reach) + 1
+            for n in range(1, 2 * reach + 2):
+                region = self.place(pl.ds(0, n))
+                copy = self.copy(region, region, 0)
+                pl.when((col >= 0) & (col < n_tx) & (rows == n))(getattr(copy, name))
+
+        def arrived(self):
+            self.wait(b - self.v, "wait_recv")
+
+        def left(self):
+            self.wait(b + self.v, "wait_send")
+
+    def fan_out(source_of, place_of, reach, span):
+        fans = [
+            Fan(source_of(v), place_of(v), reach, v).start()
+            for v in (-1, 1, -2, 2) if abs(v) <= span
+        ]
+        return fans + [
+            Remote(source_of(0), place_of(0)(reach - u), (u, 0)).start()
+            for u in (-1, 1, -2, 2) if abs(u) <= reach
+        ]
+
     def clear(o, *refs):
         @pl.when(jnp.logical_not(there(o)))
         def _():
             for ref in refs:
                 ref[...] = jnp.zeros_like(ref)
-
-    def slot(o):
-        return (o[0] + 1) * 3 + o[1] + 1
 
     clear(UP, from_up, start_up, cross_from_up, top_movie.at[pl.ds(HALF, HALF)])
     clear(DOWN, from_down, start_down, cross_from_down, bottom_movie.at[pl.ds(0, HALF)])
@@ -142,16 +180,17 @@
     clear(RIGHT, from_right, sum_from_right)
     for o in NEAR:
         if o != HERE:
-            clear(o, steps.at[slot(o)], left_sums.at[slot(o)])
+            clear(o, left_sums.at[o[1] + 1, o[0] + 1])
     for o in (UP, DOWN):
         clear(o, infos.at[0, o[0] + 1], infos.at[1, o[0] + 1], margins.at[o[0] + 1])
     for o in (LEFT, RIGHT):
         clear(o, infos.at[0, 1, o[1] + 1], infos.at[1, 1, o[1] + 1])
         clear(o, margins.at[1, o[1] + 1])
     for o in BAND:
-        clear(o, abouts.at[o[0] + 1, o[1] + 2])
-    for o in RING:
-        clear(o, far_steps.at[RING.index(o)])
+        clear(o, abouts.at[o[1] + 2, o[0] + 1])
+    for o in WIDE:
+        if o != HERE:
+            clear(o, steps.at[o[1] + 2, o[0] + 2])
 
     for copy in local[:3]:
         copy.wait()
@@ -298,16 +337,16 @@
             (tl[ROWS:] + bl[ROWS:], (tl + tr + bl + br)[:ROWS], tr[ROWS:] + br[ROWS:])
         ):
             about[i] = x[:, :F] + x[:, F:]
-        messages = []
-        for o in BAND:
-            low, high = max(0, o[1]), min(3, 3 + o[1])
-            messages.append(
-                Remote(
-                    about.at[pl.ds(low, high - low)],
-                    abouts.at[1 - o[0], 2 - o[1], pl.ds(low - o[1], high - low)], o,
-                ).start()
-            )
-        return messages
+
+        def piece(v):
+            low, high = max(0, v), min(3, 3 + v)
+            return about.at[pl.ds(low, high - low)]
+
+        def place(v):
+            low, high = max(0, v), min(3, 3 + v)
+            return lambda rows: abouts.at[2 - v, rows, pl.ds(low - v, high - low)]
+
+        return fan_out(piece, place, 1, 2)
 
     def give_back(i, l_sum, r_sum):
         sum_left[i], sum_right[i] = l_sum, r_sum
@@ -390,7 +429,7 @@
                 continue
             piece = (
                 about[o[1] + 1] if (o[0], v) == HERE
-                else abouts[o[0] + 1, v + 2, o[1] + 1]
+                else abouts[v + 2, o[0] + 1, o[1] + 1]
             )
             left_over = piece if left_over is None else left_over + piece
         return left_over
@@ -419,20 +458,14 @@
     current.append(renewed)
     own_step = renewed - previous
     step[...] = own_step
-    moves = [
-        Remote(
-            step,
-            steps.at[slot(flip(o))] if o in NEAR else far_steps.at[RING.index(flip(o))], o,
-        ).start()
-        for o in OUTWARD
-    ]
+    moves = fan_out(lambda v: step, lambda v: lambda rows: steps.at[2 - v, rows], 2, 2)
     for message in returned[1]:
         message.arrived()
     own_sum = total[rows(2)] + sum_from_left[1] + sum_from_right[1] - change[ROWS:2 * ROWS]
     left_sum[...] = own_sum
-    moves += [
-        Remote(left_sum, left_sums.at[slot(flip(o))], o).start() for o in OUTWARD if o in NEAR
-    ]
+    moves += fan_out(
+        lambda v: left_sum, lambda v: lambda rows: left_sums.at[1 - v, rows], 1, 1
+    )
     returned_late = give_back(2, *side_sums(*side_parts(3)))
     known_late = across(infos.at[1], known_late)
     lent = across(margins, lent)
@@ -454,8 +487,7 @@
         message.arrived()
     taken = {
         o: own_step if o == HERE
-        else steps[slot(o)] if o in NEAR
-        else far_steps[RING.index(o)]
+        else steps[o[1] + 2, o[0] + 2]
         for o in WIDE
     }
     moved = []
@@ -465,7 +497,7 @@
             left_over = own_sum
             last_change = change[2 * ROWS:] + nn(columns[1][3 * ROWS:], nearby)
         else:
-            left_over = left_sums[slot(o)]
+            left_over = left_sums[o[1] + 1, o[0] + 1]
         left_over = left_over - nn(weights[o], nearby)
         previous, level = known_now[o]
         renewed = stepped(previous, left_over, level)
@@ -495,7 +527,7 @@
 
 
 def body(movie, footprints, centres, traces, counts, order):
-    messages = 8 + 6 + 8 + len(BAND) + 6 + 6 + 4 + 32
+    messages = 8 + 6 + 8 + 6 + 6 + 6 + 4 + 8 + 4
     any_space = pl.BlockSpec(memory_space=pl.ANY)
     result = pl.pallas_call(
         kernel,
@@ -510,13 +542,12 @@
             *[pltpu.VMEM((K, PIX), bf16) for _ in range(8)],
             *[pltpu.VMEM((K, F), bf16) for _ in range(3)],
             pltpu.VMEM((2, 3, 3, 2 * ROWS, F), bf16),
-            pltpu.VMEM((3, ROWS, F), f32), pltpu.VMEM((3, 5, 3, ROWS, F), f32),
+            pltpu.VMEM((3, ROWS, F), f32), pltpu.VMEM((5, 3, 3, ROWS, F), f32),
             *[pltpu.VMEM((3, ROWS, F), f32) for _ in range(4)],
             *[pltpu.VMEM((3, 2 * ROWS, K), f32) for _ in range(4)],
             pltpu.VMEM((3, 3, ROWS, 9 * ROWS), f32),
-            pltpu.VMEM((ROWS, F), f32), pltpu.VMEM((9, ROWS, F), f32),
-            pltpu.VMEM((len(RING), ROWS, F), f32),
-            pltpu.VMEM((ROWS, F), f32), pltpu.VMEM((9, ROWS, F), f32),
+            pltpu.VMEM((ROWS, F), f32), pltpu.VMEM((5, 5, ROWS, F), f32),
+            pltpu.VMEM((ROWS, F), f32), pltpu.VMEM((3, 3, ROWS, F), f32),
             pltpu.VMEM((4, PIX, F), f32),
             pltpu.SemaphoreType.DMA((7,)),
             pltpu.SemaphoreType.DMA((messages,)), pltpu.SemaphoreType.DMA((messages,)),

time: 37.6 us -> 37.1 us (0.987)
  Pallas kernels: 36.3 us -> 35.8 us
    pallas_call x1, Pallas kernels: 36.3 us -> 35.8 us  [body(): pl.pallas_call(kernel, name='hals', out_shape=pltpu.VMEM((K, F), f32), in...]
where the time goes in v6:
time: 37.1 us
  Pallas kernels  35.8 us (96%)
  between operations  0.66 us (2%)
  local copies, waits for them, and re-layouts  0.61 us (2%)
    pallas_call x1, Pallas kernels, body(): pl.pallas_call(kernel, name='hals', out_shape=pltpu.VMEM((K, F), f32), in...  35.8 us

profile of v6, /device:TPU:7, one launch (start us, length us, event | category | flops | bytes accessed | tf_op | source)
XLA Modules:
  0.0 37.1 jit_solution(5702695306233193340)
XLA Ops:
  0.7 35.8 %hals.1 = f32[32,128]{1,0:T(8,128)S(1)} custom-call(bf16[32,32,128]{2,1,0:T(8,128)(2,1)} %movie.1, bf16[32,1024]{1,0:T(8,128)(2,1)} %bitcast.8, s32[2,32]{1,0:T(2,128)} %bitcast.10, bf16[32,128]{1,0:T(8,128)(2,1)} %bitcast.9, s32[1,1]{1,0:T(1,128)S(6)} %copy.9.counts_in, s32[1,32]{1,0:T(1,128)} %bitcast.11), custom_call_target="tpu_custom_call" | custom-call | tf_op jit(solution)/shard_map/hals/pallas_call | solution.py:532
  36.4 0.6 %copy.8 = f32[1,1,32,128]{3,2,1,0:T(8,128)} copy(f32[1,1,32,128]{3,2,1,0:T(8,128)S(1)} %bitcast.7) | data formatting | bytes 32768
